TPU v7x, 128 devices: a whole 4x4x4 slice. The times are simulated.
128 devices in a mesh: gz: 2 (over z_lo), gy: 4 (over z_hi, core), gx: 16 (over x, y).
Axes of the slice: x: 4, y: 4, z: 4 (z_hi: 2, z_lo: 2; z = z_hi * 2 + z_lo), core: 2. Of those that a mesh axis runs over, the one named last changes fastest.
Arguments:
- charges: float32 [262144], P(('gz', 'gy', 'gx')), may hold values from -2.5 to 2.5
- fractions: float32 [3, 262144], P(None, ('gz', 'gy', 'gx')), may hold values from 0 to 1
- base_cells: int32 [3, 262144], P(None, ('gz', 'gy', 'gx')), may hold values from 0 to 255, as said below
- counts: int32 [2, 4, 16], P('gz', 'gy', 'gx'), may hold values from 1024 to 2048, as said below
Outputs:
- forces: float32 [3, 262144], P(None, ('gz', 'gy', 'gx'))
Inputs may be any that keep to these rules, and one draw needn't show every extreme that they name: `base_cells`: atom slots of the block at gz, gy, gx have base cells inside that block's cells: x in gx*16 to gx*16 + 15, y in gy*64 to gy*64 + 63, z in gz*128 to gz*128 + 127. The first counts[b] slots of block b hold atoms, the rest are empty; some block is full in every draw.
All inputs are finite; a program needn't handle non-finite values.
Results may differ from a plain program's by a relative error of at most 0.0003.
Values sent between devices are 32-bit elements; how exact they have to be, the bound alone decides.
A program may use at most 128 MiB of HBM per device.

v0:
```python
import functools

import jax
import jax.numpy as jnp
import numpy as np
from jax import lax
from jax.experimental import pallas as pl
from jax.experimental.pallas import tpu as pltpu
from jax.sharding import PartitionSpec as P

GRID = 256
ORDER = 4
HALO = ORDER - 1
COULOMB = 332.0636
EWALD = 0.7
CX, CY, CZ = 16, 64, 128
ROWS = 72
SPAN = CX + HALO
COLUMN = 8
INTERPRET = False
F32 = jnp.float32
BF16 = jnp.bfloat16
NN = (((1,), (0,)), ((), ()))
NT = (((1,), (1,)), ((), ()))


def split_np(a):
    a = np.asarray(a, np.float32)
    high = a.astype(jnp.bfloat16)
    low = (a - high.astype(np.float32)).astype(jnp.bfloat16)
    return np.stack([high, low])


def tables():
    k = np.arange(GRID)
    half = np.arange(GRID // 2)

    def turn(first, second, length):
        angle = (first[:, None] * second[None, :] % length) * (2.0 * np.pi / length)
        return np.cos(angle), np.sin(angle)

    cos, sin = turn(k, half, GRID)
    to_kz = np.concatenate([cos, -sin], axis=1)
    twice = np.where(half > 0, 2.0, 1.0)[:, None]
    from_kz = np.concatenate([twice * cos.T, -twice * sin.T], axis=0)
    cos, sin = turn(k, k, GRID)
    real = np.concatenate([cos, sin], axis=1).reshape(64, 4, 512)
    imag = np.concatenate([-sin, cos], axis=1).reshape(64, 4, 512)
    to_ky = np.stack([real, imag], axis=1).reshape(512, 512)
    cos, sin = turn(half, half, GRID // 2)
    to_kx = np.concatenate(
        [np.concatenate([cos, sin], axis=1), np.concatenate([-sin, cos], axis=1)], axis=0
    )
    angle = half[:, None] * (2.0 * np.pi / GRID) * np.ones((1, 128))
    upper = np.arange(128)[None, :] >= 64
    twist = np.stack([np.where(upper, np.cos(angle), 1.0), np.where(upper, np.sin(angle), 0.0)])
    signed = np.where(2 * k < GRID, k, k - GRID).astype(np.float64)
    spline = 36.0 / (4.0 + 2.0 * np.cos(k * (2.0 * np.pi / GRID))) ** 2
    spline[GRID // 2] = 0.0
    decay = spline * np.exp(-np.pi**2 * signed**2 / (EWALD**2 * GRID**2))
    lanes = np.arange(128)
    kx = half[:, None] + 128 * (lanes[None, :] // 64)
    of_x = np.stack([decay[kx] * (COULOMB / (np.pi * GRID)), signed[kx] ** 2])
    kz = 64 * np.arange(2)[:, None] + lanes[None, :] % 64
    of_z = np.stack([decay[kz], signed[kz] ** 2], axis=1)
    of_y = np.stack([decay, signed**2])
    return dict(
        to_kz=split_np(to_kz),
        from_kz=split_np(from_kz),
        to_ky=split_np(to_ky),
        from_ky=split_np(to_ky.T),
        to_kx=split_np(to_kx),
        from_kx=split_np(to_kx.T),
        twist=twist.astype(np.float32),
        of_x=of_x.astype(np.float32),
        of_y=of_y.astype(np.float32),
        of_z=of_z.astype(np.float32),
    )


def halves(value):
    high = value.astype(BF16)
    return high, (value - high.astype(F32)).astype(BF16)


def dot(a, b, dims=NN):
    return lax.dot_general(a, b, dims, preferred_element_type=F32)


def dot3(a, b):
    return dot(a[0], b[0]) + (dot(a[0], b[1]) + dot(a[1], b[0]))


def spline_weights(t):
    rest = 1.0 - t
    square = t * t
    cube = square * t
    weights = (
        rest * rest * rest / 6.0,
        (3.0 * cube - 6.0 * square + 4.0) / 6.0,
        (-3.0 * cube + 3.0 * square + 3.0 * t + 1.0) / 6.0,
        cube / 6.0,
    )
    slopes = (-0.5 * rest * rest, 1.5 * square - 2.0 * t, -1.5 * square + t + 0.5, 0.5 * square)
    return weights, slopes


def place(values, lowest, rows):
    offset = lax.broadcasted_iota(jnp.int32, (rows, lowest.shape[1]), 0) - lowest
    out = jnp.where(offset == 3, values[3], 0.0)
    for i in (2, 1, 0):
        out = jnp.where(offset == i, values[i], out)
    return out


def block_index():
    return lax.axis_index("gx"), lax.axis_index("gy"), lax.axis_index("gz")


def spread_kernel(counts_ref, charges_ref, frac_ref, base_ref, out_ref, high_ref, low_ref, acc_ref, zacc_ref):
    ix, iy, iz = block_index()
    width = high_ref.shape[1]
    chunks = charges_ref.shape[1] // width
    acc_ref[...] = jnp.zeros_like(acc_ref)
    zacc_ref[...] = jnp.zeros_like(zacc_ref)

    def step(c, carry):
        at = pl.ds(pl.multiple_of(c * width, width), width)
        slot = lax.broadcasted_iota(jnp.int32, (1, width), 1) + c * width
        charge = jnp.where(slot < counts_ref[0, 0, 0], charges_ref[:, at], 0.0)
        wx, _ = spline_weights(frac_ref[0:1, at])
        wy, _ = spline_weights(frac_ref[1:2, at])
        wz, _ = spline_weights(frac_ref[2:3, at])
        wz = [w * charge for w in wz]
        low_x = base_ref[0:1, at] - ix * CX
        low_y = base_ref[1:2, at] - iy * CY
        low_z = base_ref[2:3, at] - iz * CZ
        rows_x = place(wx, low_x, 24)
        rows_y = place(wy, low_y, CZ)
        rows_z = place(wz, low_z, CZ)
        rim_z = place(wz, low_z - (CZ - HALO), 8)
        rim_row = lax.broadcasted_iota(jnp.int32, (8, 1), 0)
        rim_z = jnp.where((rim_row >= 3) & (rim_row < 6), rim_z, 0.0)
        some_y = rows_y[:ROWS]
        for x in range(SPAN):
            high, low = halves(rows_x[x : x + 1] * some_y)
            high_ref[pl.ds(x * ROWS, ROWS), :] = high
            low_ref[pl.ds(x * ROWS, ROWS), :] = low
        z_high, z_low = halves(rows_z)
        both_z = jnp.concatenate([z_high, z_low], axis=0)
        total = dot(high_ref[...], both_z, NT)
        acc_ref[...] += total[:, :CZ] + total[:, CZ:] + dot(low_ref[...], z_high, NT)
        rims = jnp.concatenate([rows_x[x : x + 1] * rim_z for x in range(SPAN)], axis=0)
        rims_high, rims_low = halves(rims)
        y_high, y_low = halves(rows_y)
        both_y = jnp.concatenate([y_high, y_low], axis=0)
        total = dot(rims_high, both_y, NT)
        zacc_ref[...] += total[:, :CZ] + total[:, CZ:] + dot(rims_low, y_high, NT)
        return carry

    lax.fori_loop(0, chunks, step, 0)
    for x in range(SPAN):
        out_ref[x, 0:64, :] = acc_ref[pl.ds(x * ROWS, 64), :]
        out_ref[x, 64:72, :] = acc_ref[pl.ds(x * ROWS + 64, 8), :] + zacc_ref[pl.ds(x * 8, 8), :]


def forward_kernel(data_ref, to_kz_ref, to_ky_ref, out_ref):
    lane = lax.broadcasted_iota(jnp.int32, (1, 128), 1)
    row = lax.broadcasted_iota(jnp.int32, (8, 128), 0)
    lower = lane < 64
    parts = []
    for x in range(2):
        planes = []
        for iz in range(2):
            pieces = []
            for iy in range(4):
                rim = jnp.where(row < HALO, data_ref[iz * 4 + (iy + 3) % 4, x, 64:72, :], 0.0)
                pieces.append(data_ref[iz * 4 + iy, x, 0:8, :] + rim)
                pieces.append(data_ref[iz * 4 + iy, x, 8:64, :])
            planes.append(jnp.concatenate(pieces, axis=0))
        rims = []
        for iz in range(2):
            tiles = [data_ref[iz * 4 + iy, x, 64:72, :] for iy in range(4)]
            turned = [pltpu.roll(tiles[1], 64, 1), pltpu.roll(tiles[3], 64, 1)]
            first = tiles[0] + jnp.where(lower, turned[1], turned[0])
            second = tiles[2] + jnp.where(lower, turned[0], turned[1])
            rims.append(jnp.concatenate([first, second], axis=1))
        rims = jnp.concatenate(rims + [jnp.zeros((112, 256), F32)], axis=0).T
        planes[1] = planes[1] + jnp.where(lane < HALO, pltpu.roll(rims, 125, 1), 0.0)
        planes[0] = planes[0] + jnp.where(lane < HALO, pltpu.roll(rims, 117, 1), 0.0)
        plane = jnp.concatenate(planes, axis=1)
        parts.append(dot3(halves(plane), (to_kz_ref[0], to_kz_ref[1])))
    rows = []
    for c in range(2):
        zero, one = (p[:, c * 128 : (c + 1) * 128] for p in parts)
        first = jnp.where(lower, zero, pltpu.roll(one, 64, 1))
        second = jnp.where(lower, pltpu.roll(zero, 64, 1), one)
        rows.append(jnp.concatenate([first, second], axis=1))
    both = jnp.concatenate(rows, axis=0)
    out = dot3((to_ky_ref[0], to_ky_ref[1]), halves(both))
    out_ref[0:64] = out[:, :128].reshape(64, 8, 128)
    out_ref[64:128] = out[:, 128:].reshape(64, 8, 128)


def middle_kernel(data_ref, to_kx_ref, from_kx_ref, twist_ref, of_x_ref, of_z_ref, of_y_ref, out_ref):
    ix, iy, iz = block_index()
    mine = ix * COLUMN + iz * 4 + iy
    half, group = mine // 64, mine % 64
    lane = lax.broadcasted_iota(jnp.int32, (1, 128), 1)
    sign = jnp.where(lane < 64, 1.0, -1.0)
    both = jnp.concatenate(
        [
            jnp.concatenate([data_ref[:, c * 4 + i, :] for i in range(4)], axis=1)
            for c in range(2)
        ],
        axis=0,
    )
    out = dot3((to_kx_ref[0], to_kx_ref[1]), halves(both))
    cos, sin = twist_ref[0], twist_ref[1]
    of_z = of_z_ref[half]
    scale_xz = of_x_ref[0] * of_z[0:1]
    square_xz = of_x_ref[1] + of_z[1:2]
    reals, imags = [], []
    for i in range(4):
        real = out[:128, i * 128 : (i + 1) * 128]
        imag = out[128:, i * 128 : (i + 1) * 128]
        real, imag = real * cos + imag * sin, imag * cos - real * sin
        real = real * sign + pltpu.roll(real, 64, 1)
        imag = imag * sign + pltpu.roll(imag, 64, 1)
        ky = group * 4 + i
        square = square_xz + of_y_ref[1, ky]
        green = jnp.where(square > 0.0, scale_xz * of_y_ref[0, ky] / jnp.maximum(square, 1.0), 0.0)
        real, imag = real * green, imag * green
        real = real * sign + pltpu.roll(real, 64, 1)
        imag = imag * sign + pltpu.roll(imag, 64, 1)
        real, imag = real * cos - imag * sin, imag * cos + real * sin
        reals.append(real)
        imags.append(imag)
    both = jnp.concatenate(
        [jnp.concatenate(reals, axis=1), jnp.concatenate(imags, axis=1)], axis=0
    )
    out = dot3((from_kx_ref[0], from_kx_ref[1]), halves(both))
    for c in range(2):
        for i in range(4):
            out_ref[:, c * 4 + i, :] = out[c * 128 : (c + 1) * 128, i * 128 : (i + 1) * 128]


def backward_kernel(data_ref, from_ky_ref, from_kz_ref, out_ref):
    lane = lax.broadcasted_iota(jnp.int32, (1, 128), 1)
    row = lax.broadcasted_iota(jnp.int32, (8, 128), 0)
    lower = lane < 64
    both = jnp.concatenate(
        [data_ref[0:64].reshape(512, 128), data_ref[64:128].reshape(512, 128)], axis=1
    )
    out = dot3((from_ky_ref[0], from_ky_ref[1]), halves(both))
    tiles = [[], []]
    for c in range(2):
        first, second = out[c * 256 : (c + 1) * 256, :128], out[c * 256 : (c + 1) * 256, 128:]
        tiles[0].append(jnp.where(lower, first, pltpu.roll(second, 64, 1)))
        tiles[1].append(jnp.where(lower, pltpu.roll(first, 64, 1), second))
    for x in range(2):
        plane = dot3(
            halves(jnp.concatenate(tiles[x], axis=1)), (from_kz_ref[0], from_kz_ref[1])
        )
        turned = [plane[:, h * 128 : (h + 1) * 128].T[:8] for h in range(2)]
        for iz in range(2):
            near = plane[:, iz * 128 : (iz + 1) * 128]
            strips = (turned[1 - iz][:, :128], turned[1 - iz][:, 128:])
            rolled = [pltpu.roll(s, 64, 1) for s in strips]
            for iy in range(4):
                after = (iy + 1) % 4
                t = iy // 2
                if iy % 2 == 0:
                    strip = strips[t]
                else:
                    strip = jnp.where(lower, rolled[t], rolled[1 - t])
                out_ref[iz * 4 + iy, x, 0:64, :] = near[iy * 64 : iy * 64 + 64]
                out_ref[iz * 4 + iy, x, 64:72, :] = jnp.where(
                    row < HALO, near[after * 64 : after * 64 + 8], pltpu.roll(strip, HALO, 0)
                )


def gather_kernel(counts_ref, charges_ref, frac_ref, base_ref, data_ref, out_ref, pot_ref, rim_ref):
    ix, iy, iz = block_index()
    width = 128
    chunks = charges_ref.shape[1] // width
    for x in range(SPAN):
        high, low = halves(data_ref[x])
        pot_ref[pl.ds(x * ROWS, ROWS), 0:128] = high
        pot_ref[pl.ds(x * ROWS, ROWS), 128:256] = low
    high, low = halves(jnp.concatenate([data_ref[x, 64:72, :] for x in range(SPAN)], axis=0))
    rim_ref[:, 0:128] = high
    rim_ref[:, 128:256] = low

    def step(c, carry):
        at = pl.ds(pl.multiple_of(c * width, width), width)
        slot = lax.broadcasted_iota(jnp.int32, (1, width), 1) + c * width
        charge = jnp.where(slot < counts_ref[0, 0, 0], charges_ref[:, at], 0.0)
        wx, sx = spline_weights(frac_ref[0:1, at])
        wy, sy = spline_weights(frac_ref[1:2, at])
        wz, sz = spline_weights(frac_ref[2:3, at])
        low_x = base_ref[0:1, at] - ix * CX
        low_y = base_ref[1:2, at] - iy * CY
        low_z = base_ref[2:3, at] - iz * CZ
        rows_x, grads_x = place(wx, low_x, 24), place(sx, low_x, 24)
        rows_y, grads_y = place(wy, low_y, CZ), place(sy, low_y, CZ)
        rows_z, grads_z = place(wz, low_z, CZ), place(sz, low_z, CZ)
        rim_row = lax.broadcasted_iota(jnp.int32, (8, 1), 0)
        inside = (rim_row >= 3) & (rim_row < 6)
        rim_low = low_z - (CZ - HALO)
        rim_rows = jnp.where(inside, place(wz, rim_low, 8), 0.0)
        rim_grads = jnp.where(inside, place(sz, rim_low, 8), 0.0)

        def folded(ref, rows, grads):
            high, low = halves(jnp.concatenate([rows, grads], axis=1))
            return dot(ref[...], jnp.concatenate([high, high], axis=0)) + dot(ref[:, 0:128], low)

        main = folded(pot_ref, rows_z, grads_z)
        rims = folded(rim_ref, rows_y, grads_y)
        force_x = jnp.zeros((8, width), F32)
        force_y = jnp.zeros((8, width), F32)
        force_z = jnp.zeros((8, width), F32)
        for x in range(SPAN):
            rim_plain = rims[x * 8 : x * 8 + 8, :width]
            rim_sloped = rims[x * 8 : x * 8 + 8, width:]
            sum_x = rim_rows * rim_plain
            sum_y = rim_rows * rim_sloped
            sum_z = rim_grads * rim_plain
            for y in range(ROWS // 8):
                low = x * ROWS + y * 8
                plain, sloped = main[low : low + 8, :width], main[low : low + 8, width:]
                near = rows_y[y * 8 : y * 8 + 8]
                sum_x += plain * near
                sum_y += plain * grads_y[y * 8 : y * 8 + 8]
                sum_z += sloped * near
            force_x += grads_x[x : x + 1] * sum_x
            force_y += rows_x[x : x + 1] * sum_y
            force_z += rows_x[x : x + 1] * sum_z
        total = [jnp.sum(f, axis=0, keepdims=True) for f in (force_x, force_y, force_z)]
        out_ref[:, at] = -charge * jnp.concatenate(total, axis=0)
        return carry

    lax.fori_loop(0, chunks, step, 0)


VMEM = pl.BlockSpec(memory_space=pltpu.VMEM)
SMEM = pl.BlockSpec(memory_space=pltpu.SMEM)


def call(kernel, shape, specs, scratch=(), limit=48 << 20):
    return pl.pallas_call(
        kernel,
        out_shape=jax.ShapeDtypeStruct(shape, F32),
        in_specs=specs,
        out_specs=VMEM,
        scratch_shapes=list(scratch),
        compiler_params=pltpu.CompilerParams(vmem_limit_bytes=limit),
        interpret=INTERPRET,
    )


def shift(value, steps):
    count = lax.axis_size("gx")
    return lax.ppermute(value, "gx", [(s, (s + steps) % count) for s in range(count)])


def per_device(charges, fractions, base_cells, counts):
    t = {name: jnp.asarray(value) for name, value in tables().items()}
    charges = charges.reshape(1, -1)
    spread = call(
        spread_kernel,
        (SPAN, ROWS, CZ),
        [SMEM, VMEM, VMEM, VMEM],
        [
            pltpu.VMEM((SPAN * ROWS, 512), BF16),
            pltpu.VMEM((SPAN * ROWS, 512), BF16),
            pltpu.VMEM((SPAN * ROWS, CZ), F32),
            pltpu.VMEM((SPAN * 8, CZ), F32),
        ],
    )
    grid = spread(counts, charges, fractions, base_cells)
    arrived = shift(grid[CX:], 1)
    grid = jnp.concatenate([grid[:HALO] + arrived, grid[HALO:CX]], axis=0)
    grid = grid.reshape(COLUMN, 2, ROWS, CZ)
    planes = lax.all_to_all(grid, ("gz", "gy"), 0, 0, tiled=True)
    forward = call(forward_kernel, (128, 8, 128), [VMEM] * 3)
    modes = forward(planes, t["to_kz"], t["to_ky"])
    modes = lax.all_to_all(modes, ("gx", "gz", "gy"), 0, 0, tiled=True)
    middle = call(middle_kernel, (128, 8, 128), [VMEM] * 6 + [SMEM])
    modes = middle(
        modes, t["to_kx"], t["from_kx"], t["twist"], t["of_x"], t["of_z"], t["of_y"]
    )
    modes = lax.all_to_all(modes, ("gx", "gz", "gy"), 0, 0, tiled=True)
    backward = call(backward_kernel, (COLUMN, 2, ROWS, CZ), [VMEM] * 3)
    planes = backward(modes, t["from_ky"], t["from_kz"])
    planes = lax.all_to_all(planes, ("gz", "gy"), 0, 0, tiled=True)
    planes = planes.reshape(CX, ROWS, CZ)
    planes = jnp.concatenate([planes, shift(planes[:HALO], -1)], axis=0)
    gather = call(
        gather_kernel,
        fractions.shape,
        [SMEM] + [VMEM] * 4,
        [pltpu.VMEM((SPAN * ROWS, 256), BF16), pltpu.VMEM((SPAN * 8, 256), BF16)],
    )
    return gather(counts, charges, fractions, base_cells, planes)


def solution(mesh):
    split = ("gz", "gy", "gx")
    return jax.shard_map(
        per_device,
        mesh=mesh,
        in_specs=(P(split), P(None, split), P(None, split), P("gz", "gy", "gx")),
        out_specs=P(None, split),
        check_vma=False,
    )
```

profile of v0, /device:TPU:1, one launch (start us, length us, event | category | flops | bytes accessed | tf_op | source)
XLA Modules:
  0.0 104.1 jit_solution(11136826410707084797)
XLA Ops:
  0.7 0.0 copy-start.8
  0.7 0.7 copy-done.8
  1.4 0.8 copy-done.10
  2.2 0.7 copy-done.12
  2.9 4.4 %shard_map.136 = f32[19,72,128]{2,1,0:T(8,128)S(1)} custom-call(s32[1,1,1]{2,1,0:T(1,128)S(6)} %copy.15.counts_ref, f32[1,2048]{1,0:T(1,128)S(1)} %bitcast.3, f32[3,2048]{1,0:T(4,128)S(1)} %copy-done.8, s32[3,2048]{1,0:T(4,128)S(1)} %copy-done.10), custom_call_target="tpu_custom_call" | custom-call | tf_op jit(solution)/shard_map/pallas_call | solution.py:381
  7.3 2.2 %collective-permute-start = (f32[3,72,128]{2,1,0:T(8,128)S(1)}, f32[3,72,128]{2,1,0:T(8,128)S(1)}, u32[]{:S(2)}, u32[]{:S(2)}) collective-permute-start(f32[3,72,128]{2,1,0:T(8,128)S(1)} %slice.17), channel_id=1, source_target_pairs={{0,1},{1,2},{2,3},{3,4},{4,5},{5,6},{6,7},{7,8},{8,9},{9,10},{10,1... | collective-permute-start | bytes 331784 | tf_op jit(solution)/shard_map/ppermute | solution.py:364
  9.5 6.3 %collective-permute-done = f32[3,72,128]{2,1,0:T(8,128)S(1)} collective-permute-done((f32[3,72,128]{2,1,0:T(8,128)S(1)}, f32[3,72,128]{2,1,0:T(8,128)S(1)}, u32[]{:S(2)}, u32[]{:S(2)}) %collective-permute-start) | collective-permute-done | bytes 110624 | tf_op jit(solution)/shard_map/ppermute | solution.py:364
  15.9 0.0 copy-start.1
  15.9 0.0 copy-start.5
  16.0 16.6 %all_to_all.20.data_ref = f32[8,2,72,128]{3,2,1,0:T(8,128)S(1)} all-to-all(f32[8,2,72,128]{3,2,1,0:T(8,128)S(1)} %bitcast.7), channel_id=1, replica_groups=mesh['gz'=2,'gy'=4,'gx'=16] {'gz','gy'}, dimensions={0} | all-to-all | bytes 1179648 | tf_op jit(solution)/shard_map/all_to_all | solution.py:385
  32.6 0.0 copy-done.5
  32.6 1.3 %shard_map.137 = f32[128,8,128]{2,1,0:T(8,128)S(1)} custom-call(f32[8,2,72,128]{3,2,1,0:T(8,128)S(1)} %all_to_all.20.data_ref, bf16[2,256,256]{2,1,0:T(8,128)(2,1)S(1)} %copy-done.5, bf16[2,512,512]{2,1,0:T(8,128)(2,1)S(1)} %copy-done.1), custom_call_target="tpu_custom_call" | custom-call | tf_op jit(solution)/shard_map/pallas_call | solution.py:387
  33.9 0.0 copy-start.3
  33.9 0.0 copy-start.4
  33.9 0.0 copy-start.6
  33.9 0.0 copy-start.7
  34.0 0.0 copy-start.14
  34.0 0.0 copy-start.15
  34.0 18.0 %all_to_all.21.data_ref = f32[128,8,128]{2,1,0:T(8,128)S(1)} all-to-all(f32[128,8,128]{2,1,0:T(8,128)S(1)} %shard_map.137), channel_id=1, replica_groups=mesh['gz'=2,'gy'=4,'gx'=16] {'gx','gz','gy'}, dimensions={0} | all-to-all | bytes 1048576 | tf_op jit(solution)/shard_map/all_to_all | solution.py:388
  52.0 0.0 copy-start
  52.0 2.1 %shard_map.138 = f32[128,8,128]{2,1,0:T(8,128)S(1)} custom-call(f32[128,8,128]{2,1,0:T(8,128)S(1)} %all_to_all.21.data_ref, bf16[2,256,256]{2,1,0:T(8,128)(2,1)S(1)} %copy-done.4, bf16[2,256,256]{2,1,0:T(8,128)(2,1)S(1)} %copy-done.3, f32[2,128,128]{2,1,0:T(8,128)S(1)} %copy-done.7, f32[2,128,128]{2,1,0:T(8,128)S(1)} %copy-done.6, ...), custom_call_target="tpu_custom_call" | custom-call | tf_op jit(solution)/shard_map/pallas_call | solution.py:390
  54.1 0.0 copy-start.2
  54.1 17.8 %all_to_all.22.data_ref = f32[128,8,128]{2,1,0:T(8,128)S(1)} all-to-all(f32[128,8,128]{2,1,0:T(8,128)S(1)} %shard_map.138), channel_id=1, replica_groups=mesh['gz'=2,'gy'=4,'gx'=16] {'gx','gz','gy'}, dimensions={0} | all-to-all | bytes 1048576 | tf_op jit(solution)/shard_map/all_to_all | solution.py:393
  72.0 1.4 %shard_map.139 = f32[8,2,72,128]{3,2,1,0:T(8,128)S(1)} custom-call(f32[128,8,128]{2,1,0:T(8,128)S(1)} %all_to_all.22.data_ref, bf16[2,512,512]{2,1,0:T(8,128)(2,1)S(1)} %copy-done, bf16[2,256,256]{2,1,0:T(8,128)(2,1)S(1)} %copy-done.2), custom_call_target="tpu_custom_call" | custom-call | tf_op jit(solution)/shard_map/pallas_call | solution.py:395
  73.4 13.8 %all_to_all.23 = f32[8,2,72,128]{3,2,1,0:T(8,128)S(1)} all-to-all(f32[8,2,72,128]{3,2,1,0:T(8,128)S(1)} %shard_map.139), channel_id=1, replica_groups=mesh['gz'=2,'gy'=4,'gx'=16] {'gz','gy'}, dimensions={0} | all-to-all | bytes 1179648 | tf_op jit(solution)/shard_map/all_to_all | solution.py:396
  87.2 0.0 copy-start.9
  87.2 0.0 copy-start.11
  87.2 0.0 copy-start.13
  87.2 1.1 %collective-permute-start.1 = (f32[3,72,128]{2,1,0:T(8,128)S(1)}, f32[3,72,128]{2,1,0:T(8,128)S(1)}, u32[]{:S(2)}, u32[]{:S(2)}) collective-permute-start(f32[3,72,128]{2,1,0:T(8,128)S(1)} %slice.19), channel_id=1, source_target_pairs={{0,15},{1,0},{2,1},{3,2},{4,3},{5,4},{6,5},{7,6},{8,7},{9,8},{10,9... | collective-permute-start | bytes 331784 | tf_op jit(solution)/shard_map/ppermute | solution.py:364
  88.3 2.6 %collective-permute-done.1 = f32[3,72,128]{2,1,0:T(8,128)S(1)} collective-permute-done((f32[3,72,128]{2,1,0:T(8,128)S(1)}, f32[3,72,128]{2,1,0:T(8,128)S(1)}, u32[]{:S(2)}, u32[]{:S(2)}) %collective-permute-start.1) | collective-permute-done | bytes 110624 | tf_op jit(solution)/shard_map/ppermute | solution.py:364
  90.9 0.1 pad_maximum_fusion.data_ref
  91.0 13.2 %shard_map.140 = f32[3,2048]{1,0:T(4,128)} custom-call(s32[1,1,1]{2,1,0:T(1,128)S(6)} %copy.15.counts_ref, f32[1,2048]{1,0:T(1,128)S(1)} %bitcast.4, f32[3,2048]{1,0:T(4,128)S(1)} %copy-done.9, s32[3,2048]{1,0:T(4,128)S(1)} %copy-done.11, f32[19,72,128]{2,1,0:T(8,128)S(1)} %pad_maximum_fusion.data_ref), custom_call_target="tpu_custom_call" | custom-call | tf_op jit(solution)/shard_map/pallas_call | solution.py:405
  (19 shorter events, 0.1 us)
Async XLA Ops:
  0.7 0.8 copy-start.8
  1.4 0.8 copy-start.10
  2.2 0.7 copy-start.12
  7.3 8.5 %collective-permute-start = (f32[3,72,128]{2,1,0:T(8,128)S(1)}, f32[3,72,128]{2,1,0:T(8,128)S(1)}, u32[]{:S(2)}, u32[]{:S(2)}) collective-permute-start(f32[3,72,128]{2,1,0:T(8,128)S(1)} %slice.17), channel_id=1, source_target_pairs={{0,1},{1,2},{2,3},{3,4},{4,5},{5,6},{6,7},{7,8},{8,9},{9,10},{10,1... | collective-permute-start | bytes 331784 | tf_op jit(solution)/shard_map/ppermute | solution.py:364
  15.9 16.7 %copy-start.1 = (bf16[2,512,512]{2,1,0:T(8,128)(2,1)S(1)}, bf16[2,512,512]{2,1,0:T(8,128)(2,1)}, u32[]{:S(2)}) copy-start(bf16[2,512,512]{2,1,0:T(8,128)(2,1)} %constant.22.clone.to_ky_ref) | copy-start | bytes 3145732
  15.9 16.7 %copy-start.5 = (bf16[2,256,256]{2,1,0:T(8,128)(2,1)S(1)}, bf16[2,256,256]{2,1,0:T(8,128)(2,1)}, u32[]{:S(2)}) copy-start(bf16[2,256,256]{2,1,0:T(8,128)(2,1)} %constant.20.clone.to_kz_ref) | copy-start | bytes 786436
  33.9 18.1 %copy-start.3 = (bf16[2,256,256]{2,1,0:T(8,128)(2,1)S(1)}, bf16[2,256,256]{2,1,0:T(8,128)(2,1)}, u32[]{:S(2)}) copy-start(bf16[2,256,256]{2,1,0:T(8,128)(2,1)} %constant.25.clone.from_kx_ref) | copy-start | bytes 786436
  33.9 18.1 %copy-start.4 = (bf16[2,256,256]{2,1,0:T(8,128)(2,1)S(1)}, bf16[2,256,256]{2,1,0:T(8,128)(2,1)}, u32[]{:S(2)}) copy-start(bf16[2,256,256]{2,1,0:T(8,128)(2,1)} %constant.24.clone.to_kx_ref) | copy-start | bytes 786436
  33.9 18.1 %copy-start.6 = (f32[2,128,128]{2,1,0:T(8,128)S(1)}, f32[2,128,128]{2,1,0:T(8,128)}, u32[]{:S(2)}) copy-start(f32[2,128,128]{2,1,0:T(8,128)} %constant.27.clone.of_x_ref) | copy-start | bytes 393220
  33.9 18.0 %copy-start.7 = (f32[2,128,128]{2,1,0:T(8,128)S(1)}, f32[2,128,128]{2,1,0:T(8,128)}, u32[]{:S(2)}) copy-start(f32[2,128,128]{2,1,0:T(8,128)} %constant.26.clone.twist_ref) | copy-start | bytes 393220
  34.0 18.0 %copy-start.14 = (f32[2,2,128]{2,1,0:T(2,128)S(1)}, f32[2,2,128]{2,1,0:T(2,128)}, u32[]{:S(2)}) copy-start(f32[2,2,128]{2,1,0:T(2,128)} %constant.29.clone.of_z_ref) | copy-start | bytes 6148
  34.0 18.0 %copy-start.15 = (f32[2,256]{1,0:T(2,128)S(1)}, f32[2,256]{1,0:T(2,128)}, u32[]{:S(2)}) copy-start(f32[2,256]{1,0:T(2,128)} %constant.28.clone.of_y_ref) | copy-start | bytes 6148
  52.0 20.0 %copy-start = (bf16[2,512,512]{2,1,0:T(8,128)(2,1)S(1)}, bf16[2,512,512]{2,1,0:T(8,128)(2,1)}, u32[]{:S(2)}) copy-start(bf16[2,512,512]{2,1,0:T(8,128)(2,1)} %constant.23.clone.from_ky_ref) | copy-start | bytes 3145732
  54.1 17.9 %copy-start.2 = (bf16[2,256,256]{2,1,0:T(8,128)(2,1)S(1)}, bf16[2,256,256]{2,1,0:T(8,128)(2,1)}, u32[]{:S(2)}) copy-start(bf16[2,256,256]{2,1,0:T(8,128)(2,1)} %constant.21.clone.from_kz_ref) | copy-start | bytes 786436
  87.2 3.8 %copy-start.9 = (f32[3,2048]{1,0:T(4,128)S(1)}, f32[3,2048]{1,0:T(4,128)}, u32[]{:S(2)}) copy-start(f32[3,2048]{1,0:T(4,128)} %frac_ref.3) | copy-start | bytes 73732
  87.2 3.8 %copy-start.11 = (s32[3,2048]{1,0:T(4,128)S(1)}, s32[3,2048]{1,0:T(4,128)}, u32[]{:S(2)}) copy-start(s32[3,2048]{1,0:T(4,128)} %base_ref.3) | copy-start | bytes 73732
  87.2 3.8 %copy-start.13 = (f32[2048]{0:T(1024)S(1)}, f32[2048]{0:T(1024)}, u32[]{:S(2)}) copy-start(f32[2048]{0:T(1024)} %param.14) | copy-start | bytes 24580
  87.2 3.7 %collective-permute-start.1 = (f32[3,72,128]{2,1,0:T(8,128)S(1)}, f32[3,72,128]{2,1,0:T(8,128)S(1)}, u32[]{:S(2)}, u32[]{:S(2)}) collective-permute-start(f32[3,72,128]{2,1,0:T(8,128)S(1)} %slice.19), channel_id=1, source_target_pairs={{0,15},{1,0},{2,1},{3,2},{4,3},{5,4},{6,5},{7,6},{8,7},{9,8},{10,9... | collective-permute-start | bytes 331784 | tf_op jit(solution)/shard_map/ppermute | solution.py:364
where the time goes:
time: 105 us; the launch traced here: 104 us
  blocking collectives  66.2 us (63%)
  Pallas kernels  22.4 us (21%)
  waiting for transfers between devices  8.93 us (9%)
  starting transfers between devices  3.25 us (3%)
  local copies, waits for them, and re-layouts  2.34 us (2%)
    all_to_all x2, blocking collectives, per_device(): modes = lax.all_to_all(modes, ('gx', 'gz', 'gy'), 0, 0, tiled=True)  35.8 us
    all_to_all x1, blocking collectives, per_device(): planes = lax.all_to_all(grid, ('gz', 'gy'), 0, 0, tiled=True)  16.6 us
    all_to_all x1, blocking collectives, per_device(): planes = lax.all_to_all(planes, ('gz', 'gy'), 0, 0, tiled=True)  13.8 us
    pallas_call x1, Pallas kernels, per_device(): return gather(counts, charges, fractions, base_cells, planes)  13.2 us
    ppermute x2, waiting for transfers between devices, shift(): lax.ppermute(value, 'gx', [(s, (s + steps) % count) for s in range(count)])  8.93 us
    pallas_call x1, Pallas kernels, per_device(): grid = spread(counts, charges, fractions, base_cells)  4.42 us
    ppermute x2, starting transfers between devices, shift(): lax.ppermute(value, 'gx', [(s, (s + steps) % count) for s in range(count)])  3.25 us
    unnamed x32, local copies, waits for them, and re-layouts  2.29 us
  transfers between devices with their start and end apart: 2, of which 2 were waited for; matrix products, arithmetic and copies ran while one was open for 0% of the time, Pallas kernels for 0%

commit v1 on v0

--- a/solution.py
+++ b/solution.py
@@ -17,7 +17,6 @@
 ROWS = 72
 SPAN = CX + HALO
 COLUMN = 8
-INTERPRET = False
 F32 = jnp.float32
 BF16 = jnp.bfloat16
 NN = (((1,), (0,)), ((), ()))
@@ -343,66 +342,156 @@
     lax.fori_loop(0, chunks, step, 0)
 
 
-VMEM = pl.BlockSpec(memory_space=pltpu.VMEM)
-SMEM = pl.BlockSpec(memory_space=pltpu.SMEM)
-
-
-def call(kernel, shape, specs, scratch=(), limit=48 << 20):
-    return pl.pallas_call(
-        kernel,
-        out_shape=jax.ShapeDtypeStruct(shape, F32),
-        in_specs=specs,
-        out_specs=VMEM,
-        scratch_shapes=list(scratch),
-        compiler_params=pltpu.CompilerParams(vmem_limit_bytes=limit),
-        interpret=INTERPRET,
-    )
-
-
-def shift(value, steps):
-    count = lax.axis_size("gx")
-    return lax.ppermute(value, "gx", [(s, (s + steps) % count) for s in range(count)])
+MESH = pl.DeviceIdType.MESH
+INPUTS = ("charges", "fractions", "base_cells")
+NAMES = ("to_kz", "to_ky", "to_kx", "twist", "of_x", "of_z", "from_kx", "from_ky", "from_kz")
+
+
+def fused_kernel(counts_ref, of_y_ref, *refs):
+    total = len(INPUTS) + len(NAMES)
+    hbm, out_ref, refs = refs[:total], refs[total], refs[total + 1 :]
+    local, refs = refs[:total], refs[total:]
+    (high_ref, low_ref, acc_ref, zacc_ref, grid_ref, rim_in_ref, planes_ref, send_ref, modes_ref,
+     send2_ref, modes2_ref, blocks_ref, near_ref, pot_ref, rim_ref,
+     load_sem, rim_send, rim_recv, a_send, a_recv, c_send, c_recv, d_send, d_recv,
+     b_send, b_recv, e_send, e_recv) = refs
+    loads = [pltpu.make_async_copy(h, v, load_sem.at[i]) for i, (h, v) in enumerate(zip(hbm, local))]
+    for load in loads:
+        load.start()
+    charges_ref, frac_ref, base_ref = local[: len(INPUTS)]
+    t = dict(zip(NAMES, local[len(INPUTS) :]))
+    ix, iy, iz = block_index()
+    count_x = lax.axis_size("gx")
+    j = iz * 4 + iy
+    mine = ix * COLUMN + j
+    after = {"gx": lax.rem(ix + 1, count_x)}
+    before = {"gx": lax.rem(ix + count_x - 1, count_x)}
+
+    def device(index):
+        low = lax.rem(index, COLUMN)
+        return {"gx": lax.div(index, COLUMN), "gz": lax.div(low, 4), "gy": lax.rem(low, 4)}
+
+    barrier = pltpu.get_barrier_semaphore()
+
+    def greet(o, carry):
+        pl.semaphore_signal(
+            barrier, inc=1, device_id=device(lax.rem(mine + o, 128)), device_id_type=MESH
+        )
+        return carry
+
+    lax.fori_loop(1, 128, greet, 0)
+    for load in loads[: len(INPUTS)]:
+        load.wait()
+    spread_kernel(counts_ref, charges_ref, frac_ref, base_ref, grid_ref, high_ref, low_ref, acc_ref, zacc_ref)
+    pl.semaphore_wait(barrier, 127)
+
+    rim = pltpu.make_async_remote_copy(
+        src_ref=grid_ref.at[pl.ds(CX, HALO)], dst_ref=rim_in_ref, send_sem=rim_send, recv_sem=rim_recv,
+        device_id=after, device_id_type=MESH,
+    )
+    rim.start()
+
+    def column(o):
+        to = lax.rem(j + o, COLUMN)
+        return to, {"gz": lax.div(to, 4), "gy": lax.rem(to, 4)}
+
+    copies = []
+    for o in range(1, COLUMN):
+        to, where = column(o)
+        copies.append((to, pltpu.make_async_remote_copy(
+            src_ref=grid_ref.at[pl.ds(2 * to, 2)], dst_ref=planes_ref.at[j],
+            send_sem=a_send.at[o], recv_sem=a_recv.at[o], device_id=where, device_id_type=MESH,
+        )))
+    for to, copy in copies:
+        pl.when(to >= 2)(copy.start)
+    rim.wait()
+    grid_ref[0:HALO] += rim_in_ref[...]
+    for to, copy in copies:
+        pl.when(to < 2)(copy.start)
+    planes_ref[pl.ds(j, 1)] = grid_ref[pl.ds(2 * j, 2)].reshape(1, 2, ROWS, CZ)
+    for load in loads[len(INPUTS) :]:
+        load.wait()
+    for _, copy in copies:
+        copy.wait()
+
+    def spray(source, target, send_sem, recv_sem):
+        def one(o, carry):
+            to = lax.rem(mine + o, 128)
+            pltpu.make_async_remote_copy(
+                src_ref=source.at[to], dst_ref=target.at[mine], send_sem=send_sem, recv_sem=recv_sem,
+                device_id=device(to), device_id_type=MESH,
+            ).start()
+            return carry
+
+        lax.fori_loop(1, 128, one, 0)
+        target[pl.ds(mine, 1)] = source[pl.ds(mine, 1)]
+        sent = source.at[pl.ds(0, 127)]
+        pltpu.make_async_copy(sent, sent, send_sem).wait()
+        got = target.at[pl.ds(0, 127)]
+        pltpu.make_async_copy(got, got, recv_sem).wait()
+
+    forward_kernel(planes_ref, t["to_kz"], t["to_ky"], send_ref)
+    spray(send_ref, modes_ref, c_send, c_recv)
+    middle_kernel(modes_ref, t["to_kx"], t["from_kx"], t["twist"], t["of_x"], t["of_z"], of_y_ref, send2_ref)
+    spray(send2_ref, modes2_ref, d_send, d_recv)
+    backward_kernel(modes2_ref, t["from_ky"], t["from_kz"], blocks_ref)
+
+    copies = []
+    for o in range(1, COLUMN):
+        to, where = column(o)
+        copies.append(pltpu.make_async_remote_copy(
+            src_ref=blocks_ref.at[to], dst_ref=near_ref.at[pl.ds(2 * j, 2)],
+            send_sem=b_send.at[o], recv_sem=b_recv.at[o], device_id=where, device_id_type=MESH,
+        ))
+    for copy in copies:
+        copy.start()
+    near_ref[pl.ds(2 * j, 2)] = blocks_ref[pl.ds(j, 1)].reshape(2, ROWS, CZ)
+    for copy in copies:
+        copy.wait()
+    rim = pltpu.make_async_remote_copy(
+        src_ref=near_ref.at[pl.ds(0, HALO)], dst_ref=near_ref.at[pl.ds(CX, HALO)],
+        send_sem=e_send, recv_sem=e_recv, device_id=before, device_id_type=MESH,
+    )
+    rim.start()
+    rim.wait()
+    gather_kernel(counts_ref, charges_ref, frac_ref, base_ref, near_ref, out_ref, pot_ref, rim_ref)
 
 
 def per_device(charges, fractions, base_cells, counts):
     t = {name: jnp.asarray(value) for name, value in tables().items()}
-    charges = charges.reshape(1, -1)
-    spread = call(
-        spread_kernel,
-        (SPAN, ROWS, CZ),
-        [SMEM, VMEM, VMEM, VMEM],
-        [
-            pltpu.VMEM((SPAN * ROWS, 512), BF16),
-            pltpu.VMEM((SPAN * ROWS, 512), BF16),
-            pltpu.VMEM((SPAN * ROWS, CZ), F32),
-            pltpu.VMEM((SPAN * 8, CZ), F32),
-        ],
-    )
-    grid = spread(counts, charges, fractions, base_cells)
-    arrived = shift(grid[CX:], 1)
-    grid = jnp.concatenate([grid[:HALO] + arrived, grid[HALO:CX]], axis=0)
-    grid = grid.reshape(COLUMN, 2, ROWS, CZ)
-    planes = lax.all_to_all(grid, ("gz", "gy"), 0, 0, tiled=True)
-    forward = call(forward_kernel, (128, 8, 128), [VMEM] * 3)
-    modes = forward(planes, t["to_kz"], t["to_ky"])
-    modes = lax.all_to_all(modes, ("gx", "gz", "gy"), 0, 0, tiled=True)
-    middle = call(middle_kernel, (128, 8, 128), [VMEM] * 6 + [SMEM])
-    modes = middle(
-        modes, t["to_kx"], t["from_kx"], t["twist"], t["of_x"], t["of_z"], t["of_y"]
-    )
-    modes = lax.all_to_all(modes, ("gx", "gz", "gy"), 0, 0, tiled=True)
-    backward = call(backward_kernel, (COLUMN, 2, ROWS, CZ), [VMEM] * 3)
-    planes = backward(modes, t["from_ky"], t["from_kz"])
-    planes = lax.all_to_all(planes, ("gz", "gy"), 0, 0, tiled=True)
-    planes = planes.reshape(CX, ROWS, CZ)
-    planes = jnp.concatenate([planes, shift(planes[:HALO], -1)], axis=0)
-    gather = call(
-        gather_kernel,
-        fractions.shape,
-        [SMEM] + [VMEM] * 4,
-        [pltpu.VMEM((SPAN * ROWS, 256), BF16), pltpu.VMEM((SPAN * 8, 256), BF16)],
-    )
-    return gather(counts, charges, fractions, base_cells, planes)
+    arrays = [charges.reshape(1, -1), fractions, base_cells] + [t[name] for name in NAMES]
+    smem = pl.BlockSpec(memory_space=pltpu.SMEM)
+    dma = pltpu.SemaphoreType.DMA
+    scratch = [pltpu.VMEM(a.shape, a.dtype) for a in arrays]
+    scratch += [
+        pltpu.VMEM((SPAN * ROWS, 512), BF16),
+        pltpu.VMEM((SPAN * ROWS, 512), BF16),
+        pltpu.VMEM((SPAN * ROWS, CZ), F32),
+        pltpu.VMEM((SPAN * 8, CZ), F32),
+        pltpu.VMEM((SPAN, ROWS, CZ), F32),
+        pltpu.VMEM((HALO, ROWS, CZ), F32),
+        pltpu.VMEM((COLUMN, 2, ROWS, CZ), F32),
+        pltpu.VMEM((128, 8, 128), F32),
+        pltpu.VMEM((128, 8, 128), F32),
+        pltpu.VMEM((128, 8, 128), F32),
+        pltpu.VMEM((128, 8, 128), F32),
+        pltpu.VMEM((COLUMN, 2, ROWS, CZ), F32),
+        pltpu.VMEM((SPAN, ROWS, CZ), F32),
+        pltpu.VMEM((SPAN * ROWS, 256), BF16),
+        pltpu.VMEM((SPAN * 8, 256), BF16),
+        dma((len(arrays),)), dma, dma, dma((COLUMN,)), dma((COLUMN,)), dma, dma, dma, dma,
+        dma((COLUMN,)), dma((COLUMN,)), dma, dma,
+    ]
+    return pl.pallas_call(
+        fused_kernel,
+        out_shape=jax.ShapeDtypeStruct(fractions.shape, F32),
+        in_specs=[smem, smem] + [pl.BlockSpec(memory_space=pl.ANY)] * len(arrays),
+        out_specs=pl.BlockSpec(memory_space=pltpu.VMEM),
+        scratch_shapes=scratch,
+        compiler_params=pltpu.CompilerParams(
+            collective_id=0, has_side_effects=True, vmem_limit_bytes=48 << 20
+        ),
+    )(counts, t["of_y"], *arrays)
 
 
 def solution(mesh):

time: 105 us -> 92.3 us (0.88)
  blocking collectives: 66.2 us -> 0 us
  Pallas kernels: 22.4 us -> 80.1 us
  waiting for transfers between devices: 8.93 us -> 0 us
  local copies, waits for them, and re-layouts: 2.34 us -> 10.9 us
  starting transfers between devices: 3.25 us -> 0 us
    all_to_all x4 -> x0, blocking collectives: 66.2 us -> none  [the longest x2 35.8 us: per_device(): modes = lax.all_to_all(modes, ('gx', 'gz', 'gy'), 0, 0, tiled=True)]
    pallas_call x5 -> x1, Pallas kernels: 22.4 us -> 80.1 us  [per_device(): pl.pallas_call(fused_kernel, out_shape=jax.ShapeDtypeStruct(fractions.sha...]
    ppermute x2 -> x0, waiting for transfers between devices: 8.93 us -> none  [shift(): lax.ppermute(value, 'gx', [(s, (s + steps) % count) for s in range(count)])]
    unnamed x32 -> x27, local copies, waits for them, and re-layouts: 2.29 us -> 10.9 us
    ppermute x2 -> x0, starting transfers between devices: 3.25 us -> none  [shift(): lax.ppermute(value, 'gx', [(s, (s + steps) % count) for s in range(count)])]
  transfers between devices with their start and end apart: 2 -> 0, of which waited for: 2 -> 0; matrix products, arithmetic and copies ran while one was open for 0% -> 0% of each run, Pallas kernels for 0% -> 0%
where the time goes in v1:
time: 92.3 us; the launch traced here: 91.7 us
  Pallas kernels  80.1 us (87%)
  local copies, waits for them, and re-layouts  10.9 us (12%)
    pallas_call x1, Pallas kernels, per_device(): pl.pallas_call(fused_kernel, out_shape=jax.ShapeDtypeStruct(fractions.sha...  80.1 us
    unnamed x27, local copies, waits for them, and re-layouts  10.9 us

profile of v1, /device:TPU:1, one launch (start us, length us, event | category | flops | bytes accessed | tf_op | source)
XLA Modules:
  0.0 91.7 jit_solution(9168036602184656859)
XLA Ops:
  0.0 0.0 copy-start.12
  0.0 0.0 copy-start.11
  0.7 0.0 copy-done.12
  0.7 0.0 copy-done.11
  0.7 0.0 copy-start
  0.7 1.2 %copy-done = bf16[2,512,512]{2,1,0:T(8,128)(2,1)S(1)} copy-done((bf16[2,512,512]{2,1,0:T(8,128)(2,1)S(1)}, bf16[2,512,512]{2,1,0:T(8,128)(2,1)}, u32[]{:S(2)}) %copy-start) | copy-done | bytes 1048600
  1.9 0.0 copy-start.1
  1.9 1.2 %copy-done.1 = bf16[2,512,512]{2,1,0:T(8,128)(2,1)S(1)} copy-done((bf16[2,512,512]{2,1,0:T(8,128)(2,1)S(1)}, bf16[2,512,512]{2,1,0:T(8,128)(2,1)}, u32[]{:S(2)}) %copy-start.1) | copy-done | bytes 1048600
  3.2 0.0 copy-start.2
  3.2 0.9 %copy-done.2 = bf16[2,256,256]{2,1,0:T(8,128)(2,1)S(1)} copy-done((bf16[2,256,256]{2,1,0:T(8,128)(2,1)S(1)}, bf16[2,256,256]{2,1,0:T(8,128)(2,1)}, u32[]{:S(2)}) %copy-start.2) | copy-done | bytes 262168
  4.1 0.0 copy-start.3
  4.1 0.9 %copy-done.3 = bf16[2,256,256]{2,1,0:T(8,128)(2,1)S(1)} copy-done((bf16[2,256,256]{2,1,0:T(8,128)(2,1)S(1)}, bf16[2,256,256]{2,1,0:T(8,128)(2,1)}, u32[]{:S(2)}) %copy-start.3) | copy-done | bytes 262168
  5.1 0.0 copy-start.4
  5.1 0.9 %copy-done.4 = bf16[2,256,256]{2,1,0:T(8,128)(2,1)S(1)} copy-done((bf16[2,256,256]{2,1,0:T(8,128)(2,1)S(1)}, bf16[2,256,256]{2,1,0:T(8,128)(2,1)}, u32[]{:S(2)}) %copy-start.4) | copy-done | bytes 262168
  6.0 0.0 copy-start.5
  6.0 0.9 %copy-done.5 = bf16[2,256,256]{2,1,0:T(8,128)(2,1)S(1)} copy-done((bf16[2,256,256]{2,1,0:T(8,128)(2,1)S(1)}, bf16[2,256,256]{2,1,0:T(8,128)(2,1)}, u32[]{:S(2)}) %copy-start.5) | copy-done | bytes 262168
  7.0 0.0 copy-start.6
  7.0 0.9 copy-done.6
  7.9 0.0 copy-start.7
  7.9 0.9 copy-done.7
  8.8 0.0 copy-start.8
  8.8 0.8 copy-done.8
  9.5 0.0 copy-start.9
  9.5 0.8 copy-done.9
  10.3 0.0 copy-start.10
  10.3 0.7 copy-done.10
  11.0 80.1 %shard_map.136 = f32[3,2048]{1,0:T(4,128)S(1)} custom-call(s32[1,1,1]{2,1,0:T(1,128)S(6)} %copy.16.counts_ref, f32[2,256]{1,0:T(2,128)S(1)} %copy-done.12, f32[1,2048]{1,0:T(1,128)S(1)} %bitcast.1, f32[3,2048]{1,0:T(4,128)S(1)} %copy-done.8, s32[3,2048]{1,0:T(4,128)S(1)} %copy-done.9, bf16[2,256,256]{2,1,0:T(8,128)(2,1)S(1)} %copy-done.5, ...), custom_call_target="tpu_custom_call" | custom-call | tf_op jit(solution)/shard_map/pallas_call | solution.py:485
  91.1 0.6 copy.17
Async XLA Ops:
  0.0 0.7 copy-start.12
  0.0 0.7 copy-start.11
  0.7 1.2 %copy-start = (bf16[2,512,512]{2,1,0:T(8,128)(2,1)S(1)}, bf16[2,512,512]{2,1,0:T(8,128)(2,1)}, u32[]{:S(2)}) copy-start(bf16[2,512,512]{2,1,0:T(8,128)(2,1)} %constant.23.clone.refs_10_) | copy-start | bytes 3145732
  1.9 1.2 %copy-start.1 = (bf16[2,512,512]{2,1,0:T(8,128)(2,1)S(1)}, bf16[2,512,512]{2,1,0:T(8,128)(2,1)}, u32[]{:S(2)}) copy-start(bf16[2,512,512]{2,1,0:T(8,128)(2,1)} %constant.22.clone.refs_4_) | copy-start | bytes 3145732
  3.2 0.9 %copy-start.2 = (bf16[2,256,256]{2,1,0:T(8,128)(2,1)S(1)}, bf16[2,256,256]{2,1,0:T(8,128)(2,1)}, u32[]{:S(2)}) copy-start(bf16[2,256,256]{2,1,0:T(8,128)(2,1)} %constant.25.clone.refs_9_) | copy-start | bytes 786436
  4.1 0.9 %copy-start.3 = (bf16[2,256,256]{2,1,0:T(8,128)(2,1)S(1)}, bf16[2,256,256]{2,1,0:T(8,128)(2,1)}, u32[]{:S(2)}) copy-start(bf16[2,256,256]{2,1,0:T(8,128)(2,1)} %constant.24.clone.refs_5_) | copy-start | bytes 786436
  5.1 0.9 %copy-start.4 = (bf16[2,256,256]{2,1,0:T(8,128)(2,1)S(1)}, bf16[2,256,256]{2,1,0:T(8,128)(2,1)}, u32[]{:S(2)}) copy-start(bf16[2,256,256]{2,1,0:T(8,128)(2,1)} %constant.21.clone.refs_11_) | copy-start | bytes 786436
  6.0 0.9 %copy-start.5 = (bf16[2,256,256]{2,1,0:T(8,128)(2,1)S(1)}, bf16[2,256,256]{2,1,0:T(8,128)(2,1)}, u32[]{:S(2)}) copy-start(bf16[2,256,256]{2,1,0:T(8,128)(2,1)} %constant.20.clone.refs_3_) | copy-start | bytes 786436
  7.0 0.9 copy-start.6
  7.9 0.9 copy-start.7
  8.8 0.8 copy-start.8
  9.5 0.8 copy-start.9
  10.3 0.7 copy-start.10

commit v2 on v1

v2 whole, which is shorter than its diff:
```python
import functools

import jax
import jax.numpy as jnp
import numpy as np
from jax import lax
from jax.experimental import pallas as pl
from jax.experimental.pallas import tpu as pltpu
from jax.sharding import PartitionSpec as P

GRID = 256
ORDER = 4
HALO = ORDER - 1
COULOMB = 332.0636
EWALD = 0.7
CX, CY, CZ = 16, 64, 128
ROWS = 72
SPAN = CX + HALO
COLUMN = 8
F32 = jnp.float32
BF16 = jnp.bfloat16
NN = (((1,), (0,)), ((), ()))
NT = (((1,), (1,)), ((), ()))


def split_np(a):
    a = np.asarray(a, np.float32)
    high = a.astype(jnp.bfloat16)
    low = (a - high.astype(np.float32)).astype(jnp.bfloat16)
    return np.stack([high, low])


def tables():
    k = np.arange(GRID)
    half = np.arange(GRID // 2)

    def turn(first, second, length):
        angle = (first[:, None] * second[None, :] % length) * (2.0 * np.pi / length)
        return np.cos(angle), np.sin(angle)

    cos, sin = turn(k, half, GRID)
    to_kz = np.concatenate([cos, -sin], axis=1)
    cos, sin = turn(k, k, GRID)
    real = np.concatenate([cos, sin], axis=1).reshape(64, 4, 512)
    imag = np.concatenate([-sin, cos], axis=1).reshape(64, 4, 512)
    to_ky = np.stack([real, imag], axis=1).reshape(512, 512)
    cos, sin = turn(half, half, GRID // 2)
    to_kx = np.concatenate(
        [np.concatenate([cos, sin], axis=1), np.concatenate([-sin, cos], axis=1)], axis=0
    )
    angle = half[:, None] * (2.0 * np.pi / GRID) * np.ones((1, 128))
    upper = np.arange(128)[None, :] >= 64
    twist = np.stack([np.where(upper, np.cos(angle), 1.0), np.where(upper, np.sin(angle), 0.0)])
    signed = np.where(2 * k < GRID, k, k - GRID).astype(np.float64)
    spline = 36.0 / (4.0 + 2.0 * np.cos(k * (2.0 * np.pi / GRID))) ** 2
    spline[GRID // 2] = 0.0
    decay = spline * np.exp(-np.pi**2 * signed**2 / (EWALD**2 * GRID**2))
    lanes = np.arange(128)
    kx = half[:, None] + 128 * (lanes[None, :] // 64)
    of_x = np.stack([decay[kx] * (COULOMB / (np.pi * GRID)), signed[kx] ** 2])
    kz = 64 * np.arange(2)[:, None] + lanes[None, :] % 64
    of_z = np.stack([decay[kz], signed[kz] ** 2], axis=1)
    of_y = np.stack([decay, signed**2])
    return dict(
        to_kz=split_np(to_kz),
        to_ky=split_np(to_ky),
        to_kx=split_np(to_kx),
        twist=twist.astype(np.float32),
        of_x=of_x.astype(np.float32),
        of_y=of_y.astype(np.float32),
        of_z=of_z.astype(np.float32),
    )


def halves(value):
    high = value.astype(BF16)
    return high, (value - high.astype(F32)).astype(BF16)


def dot(a, b, dims=NN):
    return lax.dot_general(a, b, dims, preferred_element_type=F32)


def dot3(a, b):
    return dot(
        jnp.concatenate([a[0], a[1], a[0]], axis=1), jnp.concatenate([b[0], b[0], b[1]], axis=0)
    )


def spline_weights(t):
    rest = 1.0 - t
    square = t * t
    cube = square * t
    weights = (
        rest * rest * rest / 6.0,
        (3.0 * cube - 6.0 * square + 4.0) / 6.0,
        (-3.0 * cube + 3.0 * square + 3.0 * t + 1.0) / 6.0,
        cube / 6.0,
    )
    slopes = (-0.5 * rest * rest, 1.5 * square - 2.0 * t, -1.5 * square + t + 0.5, 0.5 * square)
    return weights, slopes


def place(values, lowest, rows):
    offset = lax.broadcasted_iota(jnp.int32, (rows, lowest.shape[1]), 0) - lowest
    out = jnp.where(offset == 3, values[3], 0.0)
    for i in (2, 1, 0):
        out = jnp.where(offset == i, values[i], out)
    return out


def block_index():
    return lax.axis_index("gx"), lax.axis_index("gy"), lax.axis_index("gz")


def plane_of(iz, iy):
    return lax.rem(iy, 2) * 4 + lax.div(iy, 2) * 2 + iz


def holder_of(plane):
    return {"gz": lax.rem(plane, 2), "gy": lax.rem(lax.div(plane, 2), 2) * 2 + lax.div(plane, 4)}


def spread_rows(counts_ref, charges_ref, frac_ref, base_ref, rows_x_ref, rows_y_ref, both_z_ref, strips_ref):
    ix, iy, iz = block_index()
    slot = lax.broadcasted_iota(jnp.int32, charges_ref.shape, 1)
    charge = jnp.where(slot < counts_ref[0, 0, 0], charges_ref[...], 0.0)
    wx, _ = spline_weights(frac_ref[0:1])
    wy, _ = spline_weights(frac_ref[1:2])
    wz, _ = spline_weights(frac_ref[2:3])
    wz = [w * charge for w in wz]
    low_x = base_ref[0:1] - ix * CX
    low_y = base_ref[1:2] - iy * CY
    low_z = base_ref[2:3] - iz * CZ
    rows_x = place(wx, low_x, 24)
    rows_x_ref[...] = rows_x
    rows_y = place(wy, low_y, CZ)
    rows_y_ref[...] = rows_y[:ROWS]
    high, low = halves(place(wz, low_z, CZ))
    both_z_ref[0:CZ] = high
    both_z_ref[CZ : 2 * CZ] = low
    rim_z = place(wz, low_z - (CZ - HALO), 8)
    rim_row = lax.broadcasted_iota(jnp.int32, (8, 1), 0)
    rim_z = jnp.where((rim_row >= 3) & (rim_row < 6), rim_z, 0.0)
    rims = halves(jnp.concatenate([rows_x[x : x + 1] * rim_z for x in range(20)], axis=0))
    y_high, y_low = halves(rows_y)
    total = dot(rims[0], jnp.concatenate([y_high, y_low], axis=0), NT)
    strips_ref[...] = total[:, :CZ] + total[:, CZ:] + dot(rims[1], y_high, NT)


def spread_group(group, rows_x_ref, rows_y_ref, both_z_ref, strips_ref, high_ref, low_ref, out_ref):
    for i in range(4):
        high, low = halves(rows_x_ref[pl.ds(group * 4 + i, 1), :] * rows_y_ref[...])
        high_ref[pl.ds(i * ROWS, ROWS), :] = high
        low_ref[pl.ds(i * ROWS, ROWS), :] = low
    total = dot(high_ref[...], both_z_ref[...], NT)
    total = total[:, :CZ] + total[:, CZ:] + dot(low_ref[...], both_z_ref[0:CZ], NT)
    for i in range(4):
        x = group * 4 + i
        strip = strips_ref[pl.ds(pl.multiple_of(x * 8, 8), 8), :]
        out_ref[x, 0:64, :] = total[i * ROWS : i * ROWS + 64]
        out_ref[x, 64:72, :] = total[i * ROWS + 64 : i * ROWS + 72] + strip


def forward_kernel(data_ref, to_kz_ref, to_ky_ref, out_ref):
    lane = lax.broadcasted_iota(jnp.int32, (1, 128), 1)
    row = lax.broadcasted_iota(jnp.int32, (8, 128), 0)
    lower = lane < 64
    parts = []
    for x in range(2):
        planes = []
        for iz in range(2):
            pieces = []
            for iy in range(4):
                rim = jnp.where(row < HALO, data_ref[iz * 4 + (iy + 3) % 4, x, 64:72, :], 0.0)
                pieces.append(data_ref[iz * 4 + iy, x, 0:8, :] + rim)
                pieces.append(data_ref[iz * 4 + iy, x, 8:64, :])
            planes.append(jnp.concatenate(pieces, axis=0))
        rims = []
        for iz in range(2):
            tiles = [data_ref[iz * 4 + iy, x, 64:72, :] for iy in range(4)]
            turned = [pltpu.roll(tiles[1], 64, 1), pltpu.roll(tiles[3], 64, 1)]
            first = tiles[0] + jnp.where(lower, turned[1], turned[0])
            second = tiles[2] + jnp.where(lower, turned[0], turned[1])
            rims.append(jnp.concatenate([first, second], axis=1))
        rims = jnp.concatenate(rims + [jnp.zeros((112, 256), F32)], axis=0).T
        planes[1] = planes[1] + jnp.where(lane < HALO, pltpu.roll(rims, 125, 1), 0.0)
        planes[0] = planes[0] + jnp.where(lane < HALO, pltpu.roll(rims, 117, 1), 0.0)
        plane = jnp.concatenate(planes, axis=1)
        parts.append(dot3(halves(plane), (to_kz_ref[0], to_kz_ref[1])))
    rows = []
    for c in range(2):
        zero, one = (p[:, c * 128 : (c + 1) * 128] for p in parts)
        first = jnp.where(lower, zero, pltpu.roll(one, 64, 1))
        second = jnp.where(lower, pltpu.roll(zero, 64, 1), one)
        rows.append(jnp.concatenate([first, second], axis=1))
    both = jnp.concatenate(rows, axis=0)
    out = dot3((to_ky_ref[0], to_ky_ref[1]), halves(both))
    out_ref[0:64] = out[:, :128].reshape(64, 8, 128)
    out_ref[64:128] = out[:, 128:].reshape(64, 8, 128)


def middle_kernel(data_ref, to_kx_ref, from_kx_ref, twist_ref, of_x_ref, of_z_ref, of_y_ref, out_ref):
    ix, iy, iz = block_index()
    mine = ix * COLUMN + plane_of(iz, iy)
    half, group = mine // 64, mine % 64
    lane = lax.broadcasted_iota(jnp.int32, (1, 128), 1)
    sign = jnp.where(lane < 64, 1.0, -1.0)
    both = jnp.concatenate(
        [
            jnp.concatenate([data_ref[:, c * 4 + i, :] for i in range(4)], axis=1)
            for c in range(2)
        ],
        axis=0,
    )
    out = dot3((to_kx_ref[0], to_kx_ref[1]), halves(both))
    cos, sin = twist_ref[0], twist_ref[1]
    of_z = of_z_ref[half]
    scale_xz = of_x_ref[0] * of_z[0:1]
    square_xz = of_x_ref[1] + of_z[1:2]
    reals, imags = [], []
    for i in range(4):
        real = out[:128, i * 128 : (i + 1) * 128]
        imag = out[128:, i * 128 : (i + 1) * 128]
        real, imag = real * cos + imag * sin, imag * cos - real * sin
        real = real * sign + pltpu.roll(real, 64, 1)
        imag = imag * sign + pltpu.roll(imag, 64, 1)
        ky = group * 4 + i
        square = square_xz + of_y_ref[1, ky]
        green = jnp.where(square > 0.0, scale_xz * of_y_ref[0, ky] / jnp.maximum(square, 1.0), 0.0)
        real, imag = real * green, imag * green
        real = real * sign + pltpu.roll(real, 64, 1)
        imag = imag * sign + pltpu.roll(imag, 64, 1)
        real, imag = real * cos - imag * sin, imag * cos + real * sin
        reals.append(real)
        imags.append(imag)
    both = jnp.concatenate(
        [jnp.concatenate(reals, axis=1), jnp.concatenate(imags, axis=1)], axis=0
    )
    out = dot3((from_kx_ref[0], from_kx_ref[1]), halves(both))
    for c in range(2):
        for i in range(4):
            out_ref[:, c * 4 + i, :] = out[c * 128 : (c + 1) * 128, i * 128 : (i + 1) * 128]


def backward_kernel(data_ref, from_ky_ref, from_kz_ref, out_ref):
    lane = lax.broadcasted_iota(jnp.int32, (1, 128), 1)
    row = lax.broadcasted_iota(jnp.int32, (8, 128), 0)
    lower = lane < 64
    both = jnp.concatenate(
        [data_ref[0:64].reshape(512, 128), data_ref[64:128].reshape(512, 128)], axis=1
    )
    out = dot3((from_ky_ref[0], from_ky_ref[1]), halves(both))
    tiles = [[], []]
    for c in range(2):
        first, second = out[c * 256 : (c + 1) * 256, :128], out[c * 256 : (c + 1) * 256, 128:]
        tiles[0].append(jnp.where(lower, first, pltpu.roll(second, 64, 1)))
        tiles[1].append(jnp.where(lower, pltpu.roll(first, 64, 1), second))
    for x in range(2):
        plane = dot3(
            halves(jnp.concatenate(tiles[x], axis=1)), (from_kz_ref[0], from_kz_ref[1])
        )
        turned = [plane[:, h * 128 : (h + 1) * 128].T[:8] for h in range(2)]
        for iz in range(2):
            near = plane[:, iz * 128 : (iz + 1) * 128]
            strips = (turned[1 - iz][:, :128], turned[1 - iz][:, 128:])
            rolled = [pltpu.roll(s, 64, 1) for s in strips]
            for iy in range(4):
                after = (iy + 1) % 4
                t = iy // 2
                if iy % 2 == 0:
                    strip = strips[t]
                else:
                    strip = jnp.where(lower, rolled[t], rolled[1 - t])
                out_ref[iz * 4 + iy, x, 0:64, :] = near[iy * 64 : iy * 64 + 64]
                out_ref[iz * 4 + iy, x, 64:72, :] = jnp.where(
                    row < HALO, near[after * 64 : after * 64 + 8], pltpu.roll(strip, HALO, 0)
                )


WIDTH = 128


def gather_rows(frac_ref, base_ref, grads_x_ref, grads_y_ref, fold_z_ref, fold_y_ref, strip_ref, rows_y_ref):
    ix, iy, iz = block_index()

    def folded(rows, grads):
        high, low = halves(jnp.concatenate([rows, grads], axis=1))
        return jnp.concatenate([high, high, low], axis=0)

    def step(c, carry):
        at = pl.ds(pl.multiple_of(c * WIDTH, WIDTH), WIDTH)
        _, sx = spline_weights(frac_ref[0:1, at])
        _, sy = spline_weights(frac_ref[1:2, at])
        wz, sz = spline_weights(frac_ref[2:3, at])
        low_x = base_ref[0:1, at] - ix * CX
        low_y = base_ref[1:2, at] - iy * CY
        low_z = base_ref[2:3, at] - iz * CZ
        grads_x_ref[:, at] = place(sx, low_x, 24)
        grads_y = place(sy, low_y, ROWS)
        grads_y_ref[:, at] = grads_y
        rim_row = lax.broadcasted_iota(jnp.int32, (8, 1), 0)
        inside = (rim_row >= 3) & (rim_row < 6)
        rim_low = low_z - (CZ - HALO)
        strip_ref[0:8, at] = jnp.where(inside, place(wz, rim_low, 8), 0.0)
        strip_ref[8:16, at] = jnp.where(inside, place(sz, rim_low, 8), 0.0)
        fold_z_ref[c] = folded(place(wz, low_z, CZ), place(sz, low_z, CZ))
        pad = jnp.zeros((CZ - ROWS, WIDTH), F32)
        fold_y_ref[c] = folded(
            jnp.concatenate([rows_y_ref[:, at], pad], axis=0), jnp.concatenate([grads_y, pad], axis=0)
        )
        return carry

    lax.fori_loop(0, frac_ref.shape[1] // WIDTH, step, 0)


def gather_kernel(
    counts_ref, charges_ref, rows_x_ref, grads_x_ref, rows_y_ref, grads_y_ref, fold_z_ref, fold_y_ref,
    strip_ref, data_ref, out_ref, pot_ref, rim_ref,
):
    def spread_out(ref, at, value):
        high, low = halves(value)
        ref[at, 0:128] = high
        ref[at, 128:256] = low
        ref[at, 256:384] = high

    for x in range(SPAN):
        spread_out(pot_ref, pl.ds(x * ROWS, ROWS), data_ref[x])
    spread_out(
        rim_ref, slice(None), jnp.concatenate([data_ref[x, 64:72, :] for x in range(SPAN)], axis=0)
    )

    def step(c, carry):
        at = pl.ds(pl.multiple_of(c * WIDTH, WIDTH), WIDTH)
        slot = lax.broadcasted_iota(jnp.int32, (1, WIDTH), 1) + c * WIDTH
        charge = jnp.where(slot < counts_ref[0, 0, 0], charges_ref[:, at], 0.0)
        rows_x, grads_x = rows_x_ref[:, at], grads_x_ref[:, at]
        rows_y, grads_y = rows_y_ref[:, at], grads_y_ref[:, at]
        rim_rows, rim_grads = strip_ref[0:8, at], strip_ref[8:16, at]
        rims = dot(rim_ref[...], fold_y_ref[c])
        main = dot(pot_ref[...], fold_z_ref[c])
        force_x = jnp.zeros((8, WIDTH), F32)
        force_y = jnp.zeros((8, WIDTH), F32)
        force_z = jnp.zeros((8, WIDTH), F32)
        for x in range(SPAN):
            rim_plain = rims[x * 8 : x * 8 + 8, :WIDTH]
            rim_sloped = rims[x * 8 : x * 8 + 8, WIDTH:]
            sum_x = rim_rows * rim_plain
            sum_y = rim_rows * rim_sloped
            sum_z = rim_grads * rim_plain
            for y in range(ROWS // 8):
                low = x * ROWS + y * 8
                plain, sloped = main[low : low + 8, :WIDTH], main[low : low + 8, WIDTH:]
                near = rows_y[y * 8 : y * 8 + 8]
                sum_x += plain * near
                sum_y += plain * grads_y[y * 8 : y * 8 + 8]
                sum_z += sloped * near
            force_x += grads_x[x : x + 1] * sum_x
            force_y += rows_x[x : x + 1] * sum_y
            force_z += rows_x[x : x + 1] * sum_z
        total = [jnp.sum(f, axis=0, keepdims=True) for f in (force_x, force_y, force_z)]
        out_ref[:, at] = -charge * jnp.concatenate(total, axis=0)
        return carry

    lax.fori_loop(0, charges_ref.shape[1] // WIDTH, step, 0)


def turn_tables(to_kz_ref, to_ky_ref, to_kx_ref, from_kz_ref, from_ky_ref, from_kx_ref):
    row = lax.broadcasted_iota(jnp.int32, (GRID, 1), 0)
    twice = jnp.where(lax.rem(row, GRID // 2) == 0, 1.0, 2.0)
    for part in range(2):
        from_kz_ref[part] = (to_kz_ref[part].T.astype(F32) * twice).astype(BF16)
        from_ky_ref[part] = to_ky_ref[part].T
        from_kx_ref[part] = to_kx_ref[part].T


MESH = pl.DeviceIdType.MESH
INPUTS = ("charges", "fractions", "base_cells")
SMALL = ("counts", "of_y")
NAMES = ("to_kz", "to_ky", "to_kx", "twist", "of_x", "of_z")


FAR = sorted(
    ((a, b) for a in range(4) for b in range(4) if a or b),
    key=lambda o: -(min(o[0], 4 - o[0]) + min(o[1], 4 - o[1])),
)


def drain(ref, sem):
    pltpu.make_async_copy(ref, ref, sem).wait()


def fused_kernel(*refs):
    total = len(INPUTS) + len(SMALL) + len(NAMES)
    hbm, out_ref, refs = refs[:total], refs[total], refs[total + 1 :]
    local, refs = refs[:total], refs[total:]
    (rows_x_ref, rows_y_ref, both_z_ref, strips_ref, high_ref, low_ref, grid_ref, rim_in_ref, planes_ref,
     send_ref, modes_ref, send2_ref, modes2_ref, blocks_ref, near_ref, pot_ref, rim_ref,
     grads_x_ref, grads_y_ref, fold_z_ref, fold_y_ref, strip_ref, from_kz_ref, from_ky_ref, from_kx_ref,
     load_sem, rim_send, rim_recv, a_send, a_recv, c_send, c_recv, d_send, d_recv,
     b_send, b_recv, e_send, e_recv) = refs
    loads = [pltpu.make_async_copy(h, v, load_sem.at[i]) for i, (h, v) in enumerate(zip(hbm, local))]
    first = len(INPUTS) + len(SMALL)
    for load in loads[:first]:
        load.start()
    charges_ref, frac_ref, base_ref, counts_ref, of_y_ref = local[:first]
    t = dict(zip(NAMES, local[first:]))
    ix, iy, iz = block_index()
    count_x = lax.axis_size("gx")
    block = iz * 4 + iy
    plane = plane_of(iz, iy)
    mine = ix * COLUMN + plane
    after = {"gx": lax.rem(ix + 1, count_x)}
    before = {"gx": lax.rem(ix + count_x - 1, count_x)}
    core, height = lax.rem(iy, 2), lax.div(iy, 2) * 2 + iz
    others = []
    for up, flip in ((2, 0), (2, 1), (1, 0), (1, 1), (3, 0), (3, 1), (0, 1), (0, 0)):
        to = lax.rem(core + flip, 2) * 4 + lax.rem(height + up, 4)
        others.append((to, holder_of(to)))

    barrier = pltpu.get_barrier_semaphore()

    def everyone(action):
        def row(_, steps):
            along, across = lax.rem(steps, 4), lax.rem(lax.div(steps, 4), 4)
            to_x = lax.rem(lax.div(ix, 4) + along, 4) * 4 + lax.rem(lax.rem(ix, 4) + across, 4)
            for to, where in others:
                action(to_x * COLUMN + to, {"gx": to_x, **where})
            return lax.div(steps, 16)

        for part in (FAR[:7], FAR[7:]):
            steps = sum((a + 4 * b) << (4 * i) for i, (a, b) in enumerate(part))
            lax.fori_loop(0, len(part), row, jnp.int32(steps))
        for to, where in others[:-1]:
            action(ix * COLUMN + to, where)

    def greet(to, where):
        pl.semaphore_signal(barrier, inc=1, device_id=where, device_id_type=MESH)

    with jax.named_scope("greet"):
        everyone(greet)
    with jax.named_scope("load"):
        for load in loads[:first]:
            load.wait()
        for load in loads[first:]:
            load.start()
    spread = (rows_x_ref, rows_y_ref, both_z_ref, strips_ref)
    with jax.named_scope("rows"):
        spread_rows(counts_ref, charges_ref, frac_ref, base_ref, *spread)
    with jax.named_scope("spread4"):
        spread_group(4, *spread, high_ref, low_ref, grid_ref)
    with jax.named_scope("barwait"):
        pl.semaphore_wait(barrier, 127)
    rim = pltpu.make_async_remote_copy(
        src_ref=grid_ref.at[pl.ds(CX, HALO)], dst_ref=rim_in_ref, send_sem=rim_send, recv_sem=rim_recv,
        device_id=after, device_id_type=MESH,
    )
    rim.start()

    def give(to):
        @pl.when(to != plane)
        def _():
            pltpu.make_async_remote_copy(
                src_ref=grid_ref.at[pl.ds(2 * to, 2)], dst_ref=planes_ref.at[block],
                send_sem=a_send.at[to], recv_sem=a_recv.at[block],
                device_id=holder_of(to), device_id_type=MESH,
            ).start()

    def some(i, carry):
        group = 1 + lax.rem(i + plane, 3)
        spread_group(group, *spread, high_ref, low_ref, grid_ref)
        give(2 * group)
        give(2 * group + 1)
        return carry

    with jax.named_scope("spread123"):
        lax.fori_loop(0, 3, some, 0)
    with jax.named_scope("spread0"):
        spread_group(0, *spread, high_ref, low_ref, grid_ref)
    with jax.named_scope("rimwait"):
        rim.wait_recv()
    grid_ref[0:HALO] += rim_in_ref[...]
    give(0)
    give(1)
    planes_ref[pl.ds(block, 1)] = grid_ref[pl.ds(2 * plane, 2)].reshape(1, 2, ROWS, CZ)
    with jax.named_scope("await"):
        for load in loads[first:]:
            load.wait()
        for b in range(COLUMN):
            pl.when(b != block)(functools.partial(drain, planes_ref.at[b], a_recv.at[b]))

    def spray(source, target, send_sem, recv_sem, meanwhile):
        def one(to, where):
            pltpu.make_async_remote_copy(
                src_ref=source.at[to], dst_ref=target.at[mine], send_sem=send_sem, recv_sem=recv_sem,
                device_id=where, device_id_type=MESH,
            ).start()

        with jax.named_scope("csend"):
            everyone(one)
        target[pl.ds(mine, 1)] = source[pl.ds(mine, 1)]
        meanwhile()
        with jax.named_scope("cwait"):
            drain(target.at[pl.ds(0, 127)], recv_sem)

    with jax.named_scope("forward"):
        forward_kernel(planes_ref, t["to_kz"], t["to_ky"], send_ref)

    def prepare_back():
        with jax.named_scope("turn"):
            turn_tables(t["to_kz"], t["to_ky"], t["to_kx"], from_kz_ref, from_ky_ref, from_kx_ref)

    def prepare_gather():
        with jax.named_scope("gather_rows"):
            gather_rows(
                frac_ref, base_ref, grads_x_ref, grads_y_ref, fold_z_ref, fold_y_ref, strip_ref, rows_y_ref
            )

    spray(send_ref, modes_ref, c_send, c_recv, prepare_back)
    with jax.named_scope("middle"):
        middle_kernel(modes_ref, t["to_kx"], from_kx_ref, t["twist"], t["of_x"], t["of_z"], of_y_ref, send2_ref)
    spray(send2_ref, modes2_ref, d_send, d_recv, prepare_gather)
    with jax.named_scope("backward"):
        backward_kernel(modes2_ref, from_ky_ref, from_kz_ref, blocks_ref)

    for to, where in others[:-1]:
        to_block = where["gz"] * 4 + where["gy"]
        pltpu.make_async_remote_copy(
            src_ref=blocks_ref.at[to_block], dst_ref=near_ref.at[pl.ds(2 * plane, 2)],
            send_sem=b_send.at[to], recv_sem=b_recv.at[plane], device_id=where, device_id_type=MESH,
        ).start()
    near_ref[pl.ds(2 * plane, 2)] = blocks_ref[pl.ds(block, 1)].reshape(2, ROWS, CZ)
    rim_back = pltpu.make_async_remote_copy(
        src_ref=near_ref.at[pl.ds(0, HALO)], dst_ref=near_ref.at[pl.ds(CX, HALO)],
        send_sem=e_send, recv_sem=e_recv, device_id=before, device_id_type=MESH,
    )
    with jax.named_scope("bwait"):
        for b in range(COLUMN):
            pl.when(b != plane)(functools.partial(drain, near_ref.at[pl.ds(2 * b, 2)], b_recv.at[b]))
            if b == 1:
                rim_back.start()
    with jax.named_scope("sendwait"):
        rim.wait_send()
        rim_back.wait_send()
        for o in range(COLUMN):
            @pl.when(o != plane)
            def _():
                drain(grid_ref.at[pl.ds(2 * o, 2)], a_send.at[o])
                drain(blocks_ref.at[o], b_send.at[o])

        drain(send_ref.at[pl.ds(0, 127)], c_send)
        drain(send2_ref.at[pl.ds(0, 127)], d_send)
    with jax.named_scope("ewait"):
        rim_back.wait_recv()
    with jax.named_scope("gather"):
        gather_kernel(
            counts_ref, charges_ref, rows_x_ref, grads_x_ref, rows_y_ref, grads_y_ref, fold_z_ref,
            fold_y_ref, strip_ref, near_ref, out_ref, pot_ref, rim_ref,
        )


def per_device(charges, fractions, base_cells, counts):
    t = {name: jnp.asarray(value) for name, value in tables().items()}
    arrays = [charges.reshape(1, -1), fractions, base_cells, counts, t["of_y"]]
    arrays += [t[name] for name in NAMES]
    small = len(INPUTS) + len(SMALL)
    atoms = fractions.shape[1]
    dma = pltpu.SemaphoreType.DMA
    scratch = [
        (pltpu.SMEM if len(INPUTS) <= i < small else pltpu.VMEM)(a.shape, a.dtype)
        for i, a in enumerate(arrays)
    ]
    scratch += [
        pltpu.VMEM((24, atoms), F32),
        pltpu.VMEM((ROWS, atoms), F32),
        pltpu.VMEM((2 * CZ, atoms), BF16),
        pltpu.VMEM((160, CZ), F32),
        pltpu.VMEM((4 * ROWS, atoms), BF16),
        pltpu.VMEM((4 * ROWS, atoms), BF16),
        pltpu.VMEM((20, ROWS, CZ), F32),
        pltpu.VMEM((HALO, ROWS, CZ), F32),
        pltpu.VMEM((COLUMN, 2, ROWS, CZ), F32),
        pltpu.VMEM((128, 8, 128), F32),
        pltpu.VMEM((128, 8, 128), F32),
        pltpu.VMEM((128, 8, 128), F32),
        pltpu.VMEM((128, 8, 128), F32),
        pltpu.VMEM((COLUMN, 2, ROWS, CZ), F32),
        pltpu.VMEM((SPAN, ROWS, CZ), F32),
        pltpu.VMEM((SPAN * ROWS, 384), BF16),
        pltpu.VMEM((SPAN * 8, 384), BF16),
        pltpu.VMEM((24, atoms), F32),
        pltpu.VMEM((ROWS, atoms), F32),
        pltpu.VMEM((atoms // WIDTH, 384, 2 * WIDTH), BF16),
        pltpu.VMEM((atoms // WIDTH, 384, 2 * WIDTH), BF16),
        pltpu.VMEM((16, atoms), F32),
        pltpu.VMEM(t["to_kz"].shape, BF16),
        pltpu.VMEM(t["to_ky"].shape, BF16),
        pltpu.VMEM(t["to_kx"].shape, BF16),
        dma((len(arrays),)), dma, dma, dma((COLUMN,)), dma((COLUMN,)), dma, dma, dma, dma,
        dma((COLUMN,)), dma((COLUMN,)), dma, dma,
    ]
    return pl.pallas_call(
        fused_kernel,
        out_shape=jax.ShapeDtypeStruct(fractions.shape, F32),
        in_specs=[pl.BlockSpec(memory_space=pltpu.HBM)] * len(arrays),
        out_specs=pl.BlockSpec(memory_space=pltpu.VMEM),
        scratch_shapes=scratch,
        compiler_params=pltpu.CompilerParams(
            collective_id=0, has_side_effects=True, vmem_limit_bytes=62 << 20
        ),
    )(*arrays)


def solution(mesh):
    split = ("gz", "gy", "gx")
    return jax.shard_map(
        per_device,
        mesh=mesh,
        in_specs=(P(split), P(None, split), P(None, split), P("gz", "gy", "gx")),
        out_specs=P(None, split),
        check_vma=False,
    )
```

time: 92.3 us -> 68.2 us (0.74)
  Pallas kernels: 80.1 us -> 66 us
  local copies, waits for them, and re-layouts: 10.9 us -> 1.38 us
    pallas_call x1, Pallas kernels: 80.1 us -> 66 us  [per_device(): pl.pallas_call(fused_kernel, out_shape=jax.ShapeDtypeStruct(fractions.sha...]
    unnamed x27 -> x1, local copies, waits for them, and re-layouts: 10.9 us -> 1.38 us
where the time goes in v2:
time: 68.2 us; the launch traced here: 68 us
  Pallas kernels  66 us (97%)
  local copies, waits for them, and re-layouts  1.38 us (2%)
    pallas_call x1, Pallas kernels, per_device(): pl.pallas_call(fused_kernel, out_shape=jax.ShapeDtypeStruct(fractions.sha...  66 us
    unnamed x1, local copies, waits for them, and re-layouts  1.38 us

profile of v2, /device:TPU:1, one launch (start us, length us, event | category | flops | bytes accessed | tf_op | source)
XLA Modules:
  0.0 68.0 jit_solution(18257501606675583910)
XLA Ops:
  0.7 66.0 %shard_map.109 = f32[3,2048]{1,0:T(4,128)} custom-call(f32[1,2048]{1,0:T(1,128)} %bitcast.1, f32[3,2048]{1,0:T(4,128)} %refs_1_.1, s32[3,2048]{1,0:T(4,128)} %refs_2_.1, s32[1,1,1]{2,1,0:T(1,128)S(6)} %copy.13.refs_3_, f32[2,256]{1,0:T(2,128)} %constant.19.clone.refs_4_, bf16[2,256,256]{2,1,0:T(8,128)(2,1)} %constant.14.clone.refs_5_, ...), custom_call_target="tpu_custom_call" | custom-call | tf_op jit(solution)/shard_map/pallas_call | solution.py:602
  66.7 1.4 %copy.14 = f32[3,2048]{1,0:T(4,128)} copy(f32[3,2048]{1,0:T(4,128)} %shard_map.109) | data formatting | bytes 49152

commit v3 on v2

--- a/solution.py
+++ b/solution.py
@@ -41,9 +41,9 @@
     cos, sin = turn(k, half, GRID)
     to_kz = np.concatenate([cos, -sin], axis=1)
     cos, sin = turn(k, k, GRID)
-    real = np.concatenate([cos, sin], axis=1).reshape(64, 4, 512)
-    imag = np.concatenate([-sin, cos], axis=1).reshape(64, 4, 512)
-    to_ky = np.stack([real, imag], axis=1).reshape(512, 512)
+    real = np.concatenate([cos, sin], axis=1).reshape(64, 2, 2, 512)
+    imag = np.concatenate([-sin, cos], axis=1).reshape(64, 2, 2, 512)
+    to_ky = np.stack([real, imag], axis=2).swapaxes(0, 1).reshape(512, 512)
     cos, sin = turn(half, half, GRID // 2)
     to_kx = np.concatenate(
         [np.concatenate([cos, sin], axis=1), np.concatenate([-sin, cos], axis=1)], axis=0
@@ -87,6 +87,10 @@
     )
 
 
+def part_of(ref, *at):
+    return ref[(0, *at)], ref[(1, *at)]
+
+
 def spline_weights(t):
     rest = 1.0 - t
     square = t * t
@@ -134,8 +138,8 @@
     low_z = base_ref[2:3] - iz * CZ
     rows_x = place(wx, low_x, 24)
     rows_x_ref[...] = rows_x
-    rows_y = place(wy, low_y, CZ)
-    rows_y_ref[...] = rows_y[:ROWS]
+    rows_y = place(wy, low_y, ROWS)
+    rows_y_ref[...] = rows_y
     high, low = halves(place(wz, low_z, CZ))
     both_z_ref[0:CZ] = high
     both_z_ref[CZ : 2 * CZ] = low
@@ -143,6 +147,7 @@
     rim_row = lax.broadcasted_iota(jnp.int32, (8, 1), 0)
     rim_z = jnp.where((rim_row >= 3) & (rim_row < 6), rim_z, 0.0)
     rims = halves(jnp.concatenate([rows_x[x : x + 1] * rim_z for x in range(20)], axis=0))
+    rows_y = jnp.concatenate([rows_y, jnp.zeros((CZ - ROWS, rows_y.shape[1]), F32)], axis=0)
     y_high, y_low = halves(rows_y)
     total = dot(rims[0], jnp.concatenate([y_high, y_low], axis=0), NT)
     strips_ref[...] = total[:, :CZ] + total[:, CZ:] + dot(rims[1], y_high, NT)
@@ -162,7 +167,7 @@
         out_ref[x, 64:72, :] = total[i * ROWS + 64 : i * ROWS + 72] + strip
 
 
-def forward_kernel(data_ref, to_kz_ref, to_ky_ref, out_ref):
+def forward_kernel(data_ref, to_kz_ref, to_ky_ref, out_ref, leave):
     lane = lax.broadcasted_iota(jnp.int32, (1, 128), 1)
     row = lax.broadcasted_iota(jnp.int32, (8, 128), 0)
     lower = lane < 64
@@ -194,13 +199,15 @@
         first = jnp.where(lower, zero, pltpu.roll(one, 64, 1))
         second = jnp.where(lower, pltpu.roll(zero, 64, 1), one)
         rows.append(jnp.concatenate([first, second], axis=1))
-    both = jnp.concatenate(rows, axis=0)
-    out = dot3((to_ky_ref[0], to_ky_ref[1]), halves(both))
-    out_ref[0:64] = out[:, :128].reshape(64, 8, 128)
-    out_ref[64:128] = out[:, 128:].reshape(64, 8, 128)
-
-
-def middle_kernel(data_ref, to_kx_ref, from_kx_ref, twist_ref, of_x_ref, of_z_ref, of_y_ref, out_ref):
+    both = halves(jnp.concatenate(rows, axis=0))
+    for half in range(2):
+        out = dot3(part_of(to_ky_ref, slice(half * 256, half * 256 + 256)), both)
+        out_ref[half, 0:64] = out[:, :128].reshape(64, 4, 128)
+        out_ref[half, 64:128] = out[:, 128:].reshape(64, 4, 128)
+        leave(half)
+
+
+def middle_kernel(part, data_ref, to_kx_ref, from_kx_ref, twist_ref, of_x_ref, of_z_ref, of_y_ref, out_ref):
     ix, iy, iz = block_index()
     mine = ix * COLUMN + plane_of(iz, iy)
     half, group = mine // 64, mine % 64
@@ -208,24 +215,24 @@
     sign = jnp.where(lane < 64, 1.0, -1.0)
     both = jnp.concatenate(
         [
-            jnp.concatenate([data_ref[:, c * 4 + i, :] for i in range(4)], axis=1)
+            jnp.concatenate([data_ref[part, :, c * 2 + i, :] for i in range(2)], axis=1)
             for c in range(2)
         ],
         axis=0,
     )
-    out = dot3((to_kx_ref[0], to_kx_ref[1]), halves(both))
+    out = dot3(part_of(to_kx_ref), halves(both))
     cos, sin = twist_ref[0], twist_ref[1]
     of_z = of_z_ref[half]
     scale_xz = of_x_ref[0] * of_z[0:1]
     square_xz = of_x_ref[1] + of_z[1:2]
     reals, imags = [], []
-    for i in range(4):
+    for i in range(2):
         real = out[:128, i * 128 : (i + 1) * 128]
         imag = out[128:, i * 128 : (i + 1) * 128]
         real, imag = real * cos + imag * sin, imag * cos - real * sin
         real = real * sign + pltpu.roll(real, 64, 1)
         imag = imag * sign + pltpu.roll(imag, 64, 1)
-        ky = group * 4 + i
+        ky = group * 4 + part * 2 + i
         square = square_xz + of_y_ref[1, ky]
         green = jnp.where(square > 0.0, scale_xz * of_y_ref[0, ky] / jnp.maximum(square, 1.0), 0.0)
         real, imag = real * green, imag * green
@@ -237,29 +244,32 @@
     both = jnp.concatenate(
         [jnp.concatenate(reals, axis=1), jnp.concatenate(imags, axis=1)], axis=0
     )
-    out = dot3((from_kx_ref[0], from_kx_ref[1]), halves(both))
+    out = dot3(part_of(from_kx_ref), halves(both))
     for c in range(2):
-        for i in range(4):
-            out_ref[:, c * 4 + i, :] = out[c * 128 : (c + 1) * 128, i * 128 : (i + 1) * 128]
-
-
-def backward_kernel(data_ref, from_ky_ref, from_kz_ref, out_ref):
+        for i in range(2):
+            out_ref[part, :, c * 2 + i, :] = out[c * 128 : (c + 1) * 128, i * 128 : (i + 1) * 128]
+
+
+def backward_kernel(data_ref, from_ky_ref, from_kz_ref, out_ref, arrive):
     lane = lax.broadcasted_iota(jnp.int32, (1, 128), 1)
     row = lax.broadcasted_iota(jnp.int32, (8, 128), 0)
     lower = lane < 64
-    both = jnp.concatenate(
-        [data_ref[0:64].reshape(512, 128), data_ref[64:128].reshape(512, 128)], axis=1
-    )
-    out = dot3((from_ky_ref[0], from_ky_ref[1]), halves(both))
+    out = 0.0
+    for half in range(2):
+        arrive(half)
+        both = jnp.concatenate(
+            [data_ref[half, 0:64].reshape(256, 128), data_ref[half, 64:128].reshape(256, 128)], axis=1
+        )
+        out = out + dot3(
+            part_of(from_ky_ref, slice(None), slice(half * 256, half * 256 + 256)), halves(both)
+        )
     tiles = [[], []]
     for c in range(2):
         first, second = out[c * 256 : (c + 1) * 256, :128], out[c * 256 : (c + 1) * 256, 128:]
         tiles[0].append(jnp.where(lower, first, pltpu.roll(second, 64, 1)))
         tiles[1].append(jnp.where(lower, pltpu.roll(first, 64, 1), second))
     for x in range(2):
-        plane = dot3(
-            halves(jnp.concatenate(tiles[x], axis=1)), (from_kz_ref[0], from_kz_ref[1])
-        )
+        plane = dot3(halves(jnp.concatenate(tiles[x], axis=1)), part_of(from_kz_ref))
         turned = [plane[:, h * 128 : (h + 1) * 128].T[:8] for h in range(2)]
         for iz in range(2):
             near = plane[:, iz * 128 : (iz + 1) * 128]
@@ -279,9 +289,14 @@
 
 
 WIDTH = 128
-
-
-def gather_rows(frac_ref, base_ref, grads_x_ref, grads_y_ref, fold_z_ref, fold_y_ref, strip_ref, rows_y_ref):
+UNROLL = 4
+ORDER_UP = ((0, 0), (0, 1), (1, 0), (1, 1), (3, 0), (3, 1), (2, 0), (2, 1))
+EARLY = 6
+
+
+def gather_rows(
+    frac_ref, base_ref, rows_x_ref, both_x_ref, grads_y_ref, fold_z_ref, fold_y_ref, strip_ref, rows_y_ref
+):
     ix, iy, iz = block_index()
 
     def folded(rows, grads):
@@ -296,7 +311,8 @@
         low_x = base_ref[0:1, at] - ix * CX
         low_y = base_ref[1:2, at] - iy * CY
         low_z = base_ref[2:3, at] - iz * CZ
-        grads_x_ref[:, at] = place(sx, low_x, 24)
+        both_x_ref[c, 0:24] = rows_x_ref[:, at]
+        both_x_ref[c, 24:48] = place(sx, low_x, 24)
         grads_y = place(sy, low_y, ROWS)
         grads_y_ref[:, at] = grads_y
         rim_row = lax.broadcasted_iota(jnp.int32, (8, 1), 0)
@@ -314,55 +330,56 @@
     lax.fori_loop(0, frac_ref.shape[1] // WIDTH, step, 0)
 
 
-def gather_kernel(
-    counts_ref, charges_ref, rows_x_ref, grads_x_ref, rows_y_ref, grads_y_ref, fold_z_ref, fold_y_ref,
-    strip_ref, data_ref, out_ref, pot_ref, rim_ref,
-):
-    def spread_out(ref, at, value):
-        high, low = halves(value)
-        ref[at, 0:128] = high
-        ref[at, 128:256] = low
-        ref[at, 256:384] = high
-
-    for x in range(SPAN):
-        spread_out(pot_ref, pl.ds(x * ROWS, ROWS), data_ref[x])
-    spread_out(
-        rim_ref, slice(None), jnp.concatenate([data_ref[x, 64:72, :] for x in range(SPAN)], axis=0)
-    )
-
-    def step(c, carry):
+def stage(pot_ref, rim_ref, layers):
+    for i, layer in enumerate(layers):
+        high, low = halves(layer)
+        at = pl.ds(i * ROWS, ROWS)
+        pot_ref[at, 0:128] = high
+        pot_ref[at, 128:256] = low
+        pot_ref[at, 256:384] = high
+        at = pl.ds(i * 8, 8)
+        rim_ref[at, 0:128] = layer[64:72]
+    count = len(layers) * 8
+    high, low = halves(rim_ref[0:count, 0:128])
+    return jnp.concatenate([high, low, high], axis=1)
+
+
+def gather_part(first, last, cells, pot_ref, strips_ref, both_x_ref, rows_y_ref, grads_y_ref,
+                fold_z_ref, fold_y_ref, strip_ref, finish):
+    def one(c):
         at = pl.ds(pl.multiple_of(c * WIDTH, WIDTH), WIDTH)
-        slot = lax.broadcasted_iota(jnp.int32, (1, WIDTH), 1) + c * WIDTH
-        charge = jnp.where(slot < counts_ref[0, 0, 0], charges_ref[:, at], 0.0)
-        rows_x, grads_x = rows_x_ref[:, at], grads_x_ref[:, at]
         rows_y, grads_y = rows_y_ref[:, at], grads_y_ref[:, at]
         rim_rows, rim_grads = strip_ref[0:8, at], strip_ref[8:16, at]
-        rims = dot(rim_ref[...], fold_y_ref[c])
-        main = dot(pot_ref[...], fold_z_ref[c])
+        rims = dot(strips_ref[0 : len(cells) * 8], fold_y_ref[c])
+        main = dot(pot_ref[0 : len(cells) * ROWS], fold_z_ref[c])
         force_x = jnp.zeros((8, WIDTH), F32)
         force_y = jnp.zeros((8, WIDTH), F32)
         force_z = jnp.zeros((8, WIDTH), F32)
-        for x in range(SPAN):
-            rim_plain = rims[x * 8 : x * 8 + 8, :WIDTH]
-            rim_sloped = rims[x * 8 : x * 8 + 8, WIDTH:]
+        for i, x in enumerate(cells):
+            rim_plain = rims[i * 8 : i * 8 + 8, :WIDTH]
+            rim_sloped = rims[i * 8 : i * 8 + 8, WIDTH:]
             sum_x = rim_rows * rim_plain
             sum_y = rim_rows * rim_sloped
             sum_z = rim_grads * rim_plain
             for y in range(ROWS // 8):
-                low = x * ROWS + y * 8
+                low = i * ROWS + y * 8
                 plain, sloped = main[low : low + 8, :WIDTH], main[low : low + 8, WIDTH:]
                 near = rows_y[y * 8 : y * 8 + 8]
                 sum_x += plain * near
                 sum_y += plain * grads_y[y * 8 : y * 8 + 8]
                 sum_z += sloped * near
-            force_x += grads_x[x : x + 1] * sum_x
-            force_y += rows_x[x : x + 1] * sum_y
-            force_z += rows_x[x : x + 1] * sum_z
-        total = [jnp.sum(f, axis=0, keepdims=True) for f in (force_x, force_y, force_z)]
-        out_ref[:, at] = -charge * jnp.concatenate(total, axis=0)
+            rows_x, grads_x = both_x_ref[c, pl.ds(x, 1), :], both_x_ref[c, pl.ds(x + 24, 1), :]
+            force_x += grads_x * sum_x
+            force_y += rows_x * sum_y
+            force_z += rows_x * sum_z
+        finish(c, at, force_x, force_y, force_z)
+
+    def step(i, carry):
+        for u in range(UNROLL):
+            one(i * UNROLL + u)
         return carry
 
-    lax.fori_loop(0, charges_ref.shape[1] // WIDTH, step, 0)
+    lax.fori_loop(first // UNROLL, last // UNROLL, step, 0)
 
 
 def turn_tables(to_kz_ref, to_ky_ref, to_kx_ref, from_kz_ref, from_ky_ref, from_kx_ref):
@@ -395,8 +412,8 @@
     hbm, out_ref, refs = refs[:total], refs[total], refs[total + 1 :]
     local, refs = refs[:total], refs[total:]
     (rows_x_ref, rows_y_ref, both_z_ref, strips_ref, high_ref, low_ref, grid_ref, rim_in_ref, planes_ref,
-     send_ref, modes_ref, send2_ref, modes2_ref, blocks_ref, near_ref, pot_ref, rim_ref,
-     grads_x_ref, grads_y_ref, fold_z_ref, fold_y_ref, strip_ref, from_kz_ref, from_ky_ref, from_kx_ref,
+     send_ref, modes_ref, send2_ref, modes2_ref, blocks_ref, near_ref, far_ref, part_ref, pot_ref, rim_ref, strips2_ref,
+     both_x_ref, grads_y_ref, fold_z_ref, fold_y_ref, strip_ref, from_kz_ref, from_ky_ref, from_kx_ref,
      load_sem, rim_send, rim_recv, a_send, a_recv, c_send, c_recv, d_send, d_recv,
      b_send, b_recv, e_send, e_recv) = refs
     loads = [pltpu.make_async_copy(h, v, load_sem.at[i]) for i, (h, v) in enumerate(zip(hbm, local))]
@@ -449,14 +466,6 @@
         spread_rows(counts_ref, charges_ref, frac_ref, base_ref, *spread)
     with jax.named_scope("spread4"):
         spread_group(4, *spread, high_ref, low_ref, grid_ref)
-    with jax.named_scope("barwait"):
-        pl.semaphore_wait(barrier, 127)
-    rim = pltpu.make_async_remote_copy(
-        src_ref=grid_ref.at[pl.ds(CX, HALO)], dst_ref=rim_in_ref, send_sem=rim_send, recv_sem=rim_recv,
-        device_id=after, device_id_type=MESH,
-    )
-    rim.start()
-
     def give(to):
         @pl.when(to != plane)
         def _():
@@ -466,15 +475,30 @@
                 device_id=holder_of(to), device_id_type=MESH,
             ).start()
 
+    def group_at(i):
+        return 1 + lax.rem(i + plane, 3)
+
+    with jax.named_scope("spread1"):
+        spread_group(group_at(0), *spread, high_ref, low_ref, grid_ref)
+    with jax.named_scope("barwait"):
+        pl.semaphore_wait(barrier, 127)
+    rim = pltpu.make_async_remote_copy(
+        src_ref=grid_ref.at[pl.ds(CX, HALO)], dst_ref=rim_in_ref, send_sem=rim_send, recv_sem=rim_recv,
+        device_id=after, device_id_type=MESH,
+    )
+    rim.start()
+    give(2 * group_at(0))
+    give(2 * group_at(0) + 1)
+
     def some(i, carry):
-        group = 1 + lax.rem(i + plane, 3)
+        group = group_at(i)
         spread_group(group, *spread, high_ref, low_ref, grid_ref)
         give(2 * group)
         give(2 * group + 1)
         return carry
 
-    with jax.named_scope("spread123"):
-        lax.fori_loop(0, 3, some, 0)
+    with jax.named_scope("spread23"):
+        lax.fori_loop(1, 3, some, 0)
     with jax.named_scope("spread0"):
         spread_group(0, *spread, high_ref, low_ref, grid_ref)
     with jax.named_scope("rimwait"):
@@ -489,74 +513,129 @@
         for b in range(COLUMN):
             pl.when(b != block)(functools.partial(drain, planes_ref.at[b], a_recv.at[b]))
 
-    def spray(source, target, send_sem, recv_sem, meanwhile):
+    def spray(source, target, send_sem, recv_sem, half):
         def one(to, where):
             pltpu.make_async_remote_copy(
-                src_ref=source.at[to], dst_ref=target.at[mine], send_sem=send_sem, recv_sem=recv_sem,
-                device_id=where, device_id_type=MESH,
+                src_ref=source.at[half, to], dst_ref=target.at[half, mine], send_sem=send_sem.at[half],
+                recv_sem=recv_sem.at[half], device_id=where, device_id_type=MESH,
             ).start()
 
-        with jax.named_scope("csend"):
+        with jax.named_scope("send"):
             everyone(one)
-        target[pl.ds(mine, 1)] = source[pl.ds(mine, 1)]
-        meanwhile()
-        with jax.named_scope("cwait"):
-            drain(target.at[pl.ds(0, 127)], recv_sem)
-
-    with jax.named_scope("forward"):
-        forward_kernel(planes_ref, t["to_kz"], t["to_ky"], send_ref)
-
-    def prepare_back():
-        with jax.named_scope("turn"):
-            turn_tables(t["to_kz"], t["to_ky"], t["to_kx"], from_kz_ref, from_ky_ref, from_kx_ref)
-
-    def prepare_gather():
-        with jax.named_scope("gather_rows"):
-            gather_rows(
-                frac_ref, base_ref, grads_x_ref, grads_y_ref, fold_z_ref, fold_y_ref, strip_ref, rows_y_ref
+        target[half, pl.ds(mine, 1)] = source[half, pl.ds(mine, 1)]
+
+    def arrive(target, recv_sem, half):
+        with jax.named_scope("arrive"):
+            drain(target.at[half, pl.ds(0, 127)], recv_sem.at[half])
+
+    forward_kernel(
+        planes_ref, t["to_kz"], t["to_ky"], send_ref,
+        functools.partial(spray, send_ref, modes_ref, c_send, c_recv),
+    )
+    with jax.named_scope("turn"):
+        turn_tables(t["to_kz"], t["to_ky"], t["to_kx"], from_kz_ref, from_ky_ref, from_kx_ref)
+    for half in range(2):
+        arrive(modes_ref, c_recv, half)
+        with jax.named_scope("middle"):
+            middle_kernel(
+                half, modes_ref, t["to_kx"], from_kx_ref, t["twist"], t["of_x"], t["of_z"], of_y_ref, send2_ref
             )
-
-    spray(send_ref, modes_ref, c_send, c_recv, prepare_back)
-    with jax.named_scope("middle"):
-        middle_kernel(modes_ref, t["to_kx"], from_kx_ref, t["twist"], t["of_x"], t["of_z"], of_y_ref, send2_ref)
-    spray(send2_ref, modes2_ref, d_send, d_recv, prepare_gather)
-    with jax.named_scope("backward"):
-        backward_kernel(modes2_ref, from_ky_ref, from_kz_ref, blocks_ref)
-
-    for to, where in others[:-1]:
-        to_block = where["gz"] * 4 + where["gy"]
-        pltpu.make_async_remote_copy(
-            src_ref=blocks_ref.at[to_block], dst_ref=near_ref.at[pl.ds(2 * plane, 2)],
-            send_sem=b_send.at[to], recv_sem=b_recv.at[plane], device_id=where, device_id_type=MESH,
-        ).start()
-    near_ref[pl.ds(2 * plane, 2)] = blocks_ref[pl.ds(block, 1)].reshape(2, ROWS, CZ)
-    rim_back = pltpu.make_async_remote_copy(
-        src_ref=near_ref.at[pl.ds(0, HALO)], dst_ref=near_ref.at[pl.ds(CX, HALO)],
-        send_sem=e_send, recv_sem=e_recv, device_id=before, device_id_type=MESH,
-    )
+        spray(send2_ref, modes2_ref, d_send, d_recv, half)
+    with jax.named_scope("gather_rows"):
+        gather_rows(
+            frac_ref, base_ref, rows_x_ref, both_x_ref, grads_y_ref, fold_z_ref, fold_y_ref, strip_ref, rows_y_ref
+        )
+    backward_kernel(
+        modes2_ref, from_ky_ref, from_kz_ref, blocks_ref, functools.partial(arrive, modes2_ref, d_recv)
+    )
+
+    sends = []
+    for slot in range(1, COLUMN):
+        up, flip = ORDER_UP[slot]
+        to = lax.rem(core + flip, 2) * 4 + lax.rem(height + up, 4)
+        where = holder_of(to)
+        theirs = ORDER_UP.index(((4 - up) % 4, flip))
+        copy = pltpu.make_async_remote_copy(
+            src_ref=blocks_ref.at[where["gz"] * 4 + where["gy"]], dst_ref=near_ref.at[theirs],
+            send_sem=b_send.at[slot], recv_sem=b_recv.at[theirs], device_id=where, device_id_type=MESH,
+        )
+        copy.start()
+        sends.append(copy)
+    near_ref[0] = blocks_ref[block]
+    slot_cells = []
+    for up, flip in ORDER_UP:
+        x = 2 * (lax.rem(core + flip, 2) * 4 + lax.rem(height + up, 4))
+        slot_cells += [x, x + 1]
+
+    def slot_of(low_plane):
+        up = lax.rem(low_plane - height + 4, 4)
+        return jnp.where(up < 2, 2 * up, 10 - 2 * up) + core
+
+    rims_back = []
+    for low_plane, layers in ((0, 2), (1, 1)):
+        slot = slot_of(low_plane)
+        rims_back.append((slot, pltpu.make_async_remote_copy(
+            src_ref=near_ref.at[slot, pl.ds(0, layers)], dst_ref=far_ref.at[pl.ds(2 * low_plane, layers)],
+            send_sem=e_send.at[low_plane], recv_sem=e_recv.at[low_plane],
+            device_id=before, device_id_type=MESH,
+        )))
+    tools = (both_x_ref, rows_y_ref, grads_y_ref, fold_z_ref, fold_y_ref, strip_ref)
+    chunks = charges_ref.shape[1] // WIDTH
+
+    def keep(c, at, force_x, force_y, force_z):
+        part_ref[0, :, at] = force_x
+        part_ref[1, :, at] = force_y
+        part_ref[2, :, at] = force_z
+
+    def finish(c, at, *forces):
+        slot = lax.broadcasted_iota(jnp.int32, (1, WIDTH), 1) + c * WIDTH
+        charge = jnp.where(slot < counts_ref[0, 0, 0], charges_ref[:, at], 0.0)
+        total = [
+            jnp.sum(part_ref[d, :, at] + force, axis=0, keepdims=True) for d, force in enumerate(forces)
+        ]
+        out_ref[:, at] = -charge * jnp.concatenate(total, axis=0)
+
     with jax.named_scope("bwait"):
-        for b in range(COLUMN):
-            pl.when(b != plane)(functools.partial(drain, near_ref.at[pl.ds(2 * b, 2)], b_recv.at[b]))
-            if b == 1:
-                rim_back.start()
+        for slot in range(1, EARLY):
+            drain(near_ref.at[slot], b_recv.at[slot])
+        for slot, copy in rims_back:
+            pl.when(slot < EARLY)(copy.start)
+    with jax.named_scope("stage1"):
+        strips2_ref[0 : EARLY * 16] = stage(
+            pot_ref, rim_ref, [near_ref[slot, i] for slot in range(EARLY) for i in range(2)]
+        )
+    with jax.named_scope("gather1"):
+        gather_part(0, chunks // 2, slot_cells[: 2 * EARLY], pot_ref, strips2_ref, *tools, keep)
+    with jax.named_scope("bwait2"):
+        for slot in range(EARLY, COLUMN):
+            drain(near_ref.at[slot], b_recv.at[slot])
+        for slot, copy in rims_back:
+            pl.when(slot >= EARLY)(copy.start)
+    with jax.named_scope("gather2"):
+        gather_part(chunks // 2, chunks, slot_cells[: 2 * EARLY], pot_ref, strips2_ref, *tools, keep)
     with jax.named_scope("sendwait"):
         rim.wait_send()
-        rim_back.wait_send()
         for o in range(COLUMN):
             @pl.when(o != plane)
             def _():
                 drain(grid_ref.at[pl.ds(2 * o, 2)], a_send.at[o])
-                drain(blocks_ref.at[o], b_send.at[o])
-
-        drain(send_ref.at[pl.ds(0, 127)], c_send)
-        drain(send2_ref.at[pl.ds(0, 127)], d_send)
+
+        for half in range(2):
+            drain(send_ref.at[half, pl.ds(0, 127)], c_send.at[half])
+            drain(send2_ref.at[half, pl.ds(0, 127)], d_send.at[half])
+        for copy in sends:
+            copy.wait_send()
     with jax.named_scope("ewait"):
-        rim_back.wait_recv()
-    with jax.named_scope("gather"):
-        gather_kernel(
-            counts_ref, charges_ref, rows_x_ref, grads_x_ref, rows_y_ref, grads_y_ref, fold_z_ref,
-            fold_y_ref, strip_ref, near_ref, out_ref, pot_ref, rim_ref,
-        )
+        for _, copy in rims_back:
+            copy.wait_send()
+            copy.wait_recv()
+    with jax.named_scope("stage3"):
+        late = [near_ref[slot, i] for slot in range(EARLY, COLUMN) for i in range(2)]
+        late += [far_ref[i] for i in range(HALO)]
+        strips2_ref[0 : len(late) * 8] = stage(pot_ref, rim_ref, late)
+    with jax.named_scope("gather3"):
+        cells = slot_cells[2 * EARLY :] + [CX, CX + 1, CX + 2]
+        gather_part(0, chunks, cells, pot_ref, strips2_ref, *tools, finish)
 
 
 def per_device(charges, fractions, base_cells, counts):
@@ -580,15 +659,18 @@
         pltpu.VMEM((20, ROWS, CZ), F32),
         pltpu.VMEM((HALO, ROWS, CZ), F32),
         pltpu.VMEM((COLUMN, 2, ROWS, CZ), F32),
-        pltpu.VMEM((128, 8, 128), F32),
-        pltpu.VMEM((128, 8, 128), F32),
-        pltpu.VMEM((128, 8, 128), F32),
-        pltpu.VMEM((128, 8, 128), F32),
+        pltpu.VMEM((2, 128, 4, 128), F32),
+        pltpu.VMEM((2, 128, 4, 128), F32),
+        pltpu.VMEM((2, 128, 4, 128), F32),
+        pltpu.VMEM((2, 128, 4, 128), F32),
         pltpu.VMEM((COLUMN, 2, ROWS, CZ), F32),
-        pltpu.VMEM((SPAN, ROWS, CZ), F32),
-        pltpu.VMEM((SPAN * ROWS, 384), BF16),
-        pltpu.VMEM((SPAN * 8, 384), BF16),
-        pltpu.VMEM((24, atoms), F32),
+        pltpu.VMEM((COLUMN, 2, ROWS, CZ), F32),
+        pltpu.VMEM((HALO, ROWS, CZ), F32),
+        pltpu.VMEM((3, 8, atoms), F32),
+        pltpu.VMEM((2 * EARLY * ROWS, 384), BF16),
+        pltpu.VMEM((2 * EARLY * 8, 128), F32),
+        pltpu.VMEM((2 * EARLY * 8, 384), BF16),
+        pltpu.VMEM((atoms // WIDTH, 48, WIDTH), F32),
         pltpu.VMEM((ROWS, atoms), F32),
         pltpu.VMEM((atoms // WIDTH, 384, 2 * WIDTH), BF16),
         pltpu.VMEM((atoms // WIDTH, 384, 2 * WIDTH), BF16),
@@ -596,8 +678,8 @@
         pltpu.VMEM(t["to_kz"].shape, BF16),
         pltpu.VMEM(t["to_ky"].shape, BF16),
         pltpu.VMEM(t["to_kx"].shape, BF16),
-        dma((len(arrays),)), dma, dma, dma((COLUMN,)), dma((COLUMN,)), dma, dma, dma, dma,
-        dma((COLUMN,)), dma((COLUMN,)), dma, dma,
+        dma((len(arrays),)), dma, dma, dma((COLUMN,)), dma((COLUMN,)), dma((2,)), dma((2,)), dma((2,)), dma((2,)),
+        dma((COLUMN,)), dma((COLUMN,)), dma((2,)), dma((2,)),
     ]
     return pl.pallas_call(
         fused_kernel,

time: 68.2 us -> 59.4 us (0.87)
  Pallas kernels: 66 us -> 56.6 us
    pallas_call x1, Pallas kernels: 66 us -> 56.6 us  [per_device(): pl.pallas_call(fused_kernel, out_shape=jax.ShapeDtypeStruct(fractions.sha...]
where the time goes in v3:
time: 59.4 us; the launch traced here: 58.6 us
  Pallas kernels  56.6 us (95%)
  local copies, waits for them, and re-layouts  1.38 us (2%)
  between operations  0.66 us (1%)
    pallas_call x1, Pallas kernels, per_device(): pl.pallas_call(fused_kernel, out_shape=jax.ShapeDtypeStruct(fractions.sha...  56.6 us
    unnamed x1, local copies, waits for them, and re-layouts  1.38 us

profile of v3, /device:TPU:1, one launch (start us, length us, event | category | flops | bytes accessed | tf_op | source)
XLA Modules:
  0.0 58.6 jit_solution(9227032569729730376)
XLA Ops:
  0.7 56.6 %shard_map.109 = f32[3,2048]{1,0:T(4,128)} custom-call(f32[1,2048]{1,0:T(1,128)} %bitcast.1, f32[3,2048]{1,0:T(4,128)} %refs_1_.1, s32[3,2048]{1,0:T(4,128)} %refs_2_.1, s32[1,1,1]{2,1,0:T(1,128)S(6)} %copy.13.refs_3_, f32[2,256]{1,0:T(2,128)} %constant.19.clone.refs_4_, bf16[2,256,256]{2,1,0:T(8,128)(2,1)} %constant.14.clone.refs_5_, ...), custom_call_target="tpu_custom_call" | custom-call | tf_op jit(solution)/shard_map/pallas_call | solution.py:684
  57.2 1.4 %copy.14 = f32[3,2048]{1,0:T(4,128)} copy(f32[3,2048]{1,0:T(4,128)} %shard_map.109) | data formatting | bytes 49152

commit v4 on v3

--- a/solution.py
+++ b/solution.py
@@ -125,32 +125,43 @@
     return {"gz": lax.rem(plane, 2), "gy": lax.rem(lax.div(plane, 2), 2) * 2 + lax.div(plane, 4)}
 
 
-def spread_rows(counts_ref, charges_ref, frac_ref, base_ref, rows_x_ref, rows_y_ref, both_z_ref, strips_ref):
+def spread_rows(counts_ref, charges_ref, frac_ref, base_ref, rows_x_ref, rows_y_ref, both_z_ref, strips_ref,
+                both_y_ref, high_ref, low_ref):
     ix, iy, iz = block_index()
-    slot = lax.broadcasted_iota(jnp.int32, charges_ref.shape, 1)
-    charge = jnp.where(slot < counts_ref[0, 0, 0], charges_ref[...], 0.0)
-    wx, _ = spline_weights(frac_ref[0:1])
-    wy, _ = spline_weights(frac_ref[1:2])
-    wz, _ = spline_weights(frac_ref[2:3])
-    wz = [w * charge for w in wz]
-    low_x = base_ref[0:1] - ix * CX
-    low_y = base_ref[1:2] - iy * CY
-    low_z = base_ref[2:3] - iz * CZ
-    rows_x = place(wx, low_x, 24)
-    rows_x_ref[...] = rows_x
-    rows_y = place(wy, low_y, ROWS)
-    rows_y_ref[...] = rows_y
-    high, low = halves(place(wz, low_z, CZ))
-    both_z_ref[0:CZ] = high
-    both_z_ref[CZ : 2 * CZ] = low
-    rim_z = place(wz, low_z - (CZ - HALO), 8)
+    width = 512
     rim_row = lax.broadcasted_iota(jnp.int32, (8, 1), 0)
-    rim_z = jnp.where((rim_row >= 3) & (rim_row < 6), rim_z, 0.0)
-    rims = halves(jnp.concatenate([rows_x[x : x + 1] * rim_z for x in range(20)], axis=0))
-    rows_y = jnp.concatenate([rows_y, jnp.zeros((CZ - ROWS, rows_y.shape[1]), F32)], axis=0)
-    y_high, y_low = halves(rows_y)
-    total = dot(rims[0], jnp.concatenate([y_high, y_low], axis=0), NT)
-    strips_ref[...] = total[:, :CZ] + total[:, CZ:] + dot(rims[1], y_high, NT)
+    inside = (rim_row >= 3) & (rim_row < 6)
+
+    for c in range(charges_ref.shape[1] // width):
+        at = pl.ds(c * width, width)
+        slot = lax.broadcasted_iota(jnp.int32, (1, width), 1) + c * width
+        charge = jnp.where(slot < counts_ref[0, 0, 0], charges_ref[:, at], 0.0)
+        wx, _ = spline_weights(frac_ref[0:1, at])
+        wy, _ = spline_weights(frac_ref[1:2, at])
+        wz, _ = spline_weights(frac_ref[2:3, at])
+        wz = [w * charge for w in wz]
+        low_z = base_ref[2:3, at] - iz * CZ
+        rows_x = place(wx, base_ref[0:1, at] - ix * CX, 24)
+        rows_x_ref[:, at] = rows_x
+        rows_y = place(wy, base_ref[1:2, at] - iy * CY, ROWS)
+        rows_y_ref[:, at] = rows_y
+        high, low = halves(rows_y)
+        both_y_ref[0:ROWS, at] = high
+        both_y_ref[ROWS : 2 * ROWS, at] = low
+        high, low = halves(place(wz, low_z, CZ))
+        both_z_ref[0:CZ, at] = high
+        both_z_ref[CZ : 2 * CZ, at] = low
+        rim_z = jnp.where(inside, place(wz, low_z - (CZ - HALO), 8), 0.0)
+        high, low = halves(jnp.concatenate([rows_x[x : x + 1] * rim_z for x in range(20)], axis=0))
+        high_ref[0:160, at] = high
+        low_ref[0:160, at] = low
+    pad = jnp.zeros((256 - 2 * ROWS, both_y_ref.shape[1]), BF16)
+    total = dot(high_ref[0:160], jnp.concatenate([both_y_ref[...], pad], axis=0), NT)
+    pad = jnp.zeros((CZ - ROWS, both_y_ref.shape[1]), BF16)
+    more = dot(low_ref[0:160], jnp.concatenate([both_y_ref[0:ROWS], pad], axis=0), NT)
+    strips_ref[...] = jnp.concatenate(
+        [total[:, :ROWS] + total[:, ROWS : 2 * ROWS], jnp.zeros((160, CZ - ROWS), F32)], axis=1
+    ) + more
 
 
 def spread_group(group, rows_x_ref, rows_y_ref, both_z_ref, strips_ref, high_ref, low_ref, out_ref):
@@ -202,8 +213,9 @@
     both = halves(jnp.concatenate(rows, axis=0))
     for half in range(2):
         out = dot3(part_of(to_ky_ref, slice(half * 256, half * 256 + 256)), both)
-        out_ref[half, 0:64] = out[:, :128].reshape(64, 4, 128)
-        out_ref[half, 64:128] = out[:, 128:].reshape(64, 4, 128)
+        flat = out_ref.reshape(2, 512, 128)
+        flat[half, 0:256] = out[:, :128]
+        flat[half, 256:512] = out[:, 128:]
         leave(half)
 
 
@@ -213,9 +225,10 @@
     half, group = mine // 64, mine % 64
     lane = lax.broadcasted_iota(jnp.int32, (1, 128), 1)
     sign = jnp.where(lane < 64, 1.0, -1.0)
+    flat = data_ref.reshape(2, 512, 128)
     both = jnp.concatenate(
         [
-            jnp.concatenate([data_ref[part, :, c * 2 + i, :] for i in range(2)], axis=1)
+            jnp.concatenate([flat[part, pl.ds(c * 2 + i, 128, stride=4), :] for i in range(2)], axis=1)
             for c in range(2)
         ],
         axis=0,
@@ -245,9 +258,10 @@
         [jnp.concatenate(reals, axis=1), jnp.concatenate(imags, axis=1)], axis=0
     )
     out = dot3(part_of(from_kx_ref), halves(both))
+    flat = out_ref.reshape(2, 512, 128)
     for c in range(2):
         for i in range(2):
-            out_ref[part, :, c * 2 + i, :] = out[c * 128 : (c + 1) * 128, i * 128 : (i + 1) * 128]
+            flat[part, pl.ds(c * 2 + i, 128, stride=4), :] = out[c * 128 : (c + 1) * 128, i * 128 : (i + 1) * 128]
 
 
 def backward_kernel(data_ref, from_ky_ref, from_kz_ref, out_ref, arrive):
@@ -257,9 +271,8 @@
     out = 0.0
     for half in range(2):
         arrive(half)
-        both = jnp.concatenate(
-            [data_ref[half, 0:64].reshape(256, 128), data_ref[half, 64:128].reshape(256, 128)], axis=1
-        )
+        flat = data_ref.reshape(2, 512, 128)
+        both = jnp.concatenate([flat[half, 0:256], flat[half, 256:512]], axis=1)
         out = out + dot3(
             part_of(from_ky_ref, slice(None), slice(half * 256, half * 256 + 256)), halves(both)
         )
@@ -294,73 +307,62 @@
 EARLY = 6
 
 
-def gather_rows(
-    frac_ref, base_ref, rows_x_ref, both_x_ref, grads_y_ref, fold_z_ref, fold_y_ref, strip_ref, rows_y_ref
-):
+def gather_rows(frac_ref, base_ref, rows_x_ref, both_x_ref, grads_y_ref, fold_z_ref):
     ix, iy, iz = block_index()
-
-    def folded(rows, grads):
-        high, low = halves(jnp.concatenate([rows, grads], axis=1))
-        return jnp.concatenate([high, high, low], axis=0)
+    rim_row = lax.broadcasted_iota(jnp.int32, (8, 1), 0)
+    inside = (rim_row >= 3) & (rim_row < 6)
 
     def step(c, carry):
         at = pl.ds(pl.multiple_of(c * WIDTH, WIDTH), WIDTH)
         _, sx = spline_weights(frac_ref[0:1, at])
         _, sy = spline_weights(frac_ref[1:2, at])
         wz, sz = spline_weights(frac_ref[2:3, at])
-        low_x = base_ref[0:1, at] - ix * CX
-        low_y = base_ref[1:2, at] - iy * CY
         low_z = base_ref[2:3, at] - iz * CZ
         both_x_ref[c, 0:24] = rows_x_ref[:, at]
-        both_x_ref[c, 24:48] = place(sx, low_x, 24)
-        grads_y = place(sy, low_y, ROWS)
-        grads_y_ref[:, at] = grads_y
-        rim_row = lax.broadcasted_iota(jnp.int32, (8, 1), 0)
-        inside = (rim_row >= 3) & (rim_row < 6)
+        both_x_ref[c, 24:48] = place(sx, base_ref[0:1, at] - ix * CX, 24)
+        grads_y_ref[:, at] = place(sy, base_ref[1:2, at] - iy * CY, ROWS)
+        high, low = halves(jnp.concatenate([place(wz, low_z, CZ), place(sz, low_z, CZ)], axis=1))
+        fold_z_ref[c, 0:128] = high
+        fold_z_ref[c, 128:256] = high
+        fold_z_ref[c, 256:384] = low
         rim_low = low_z - (CZ - HALO)
-        strip_ref[0:8, at] = jnp.where(inside, place(wz, rim_low, 8), 0.0)
-        strip_ref[8:16, at] = jnp.where(inside, place(sz, rim_low, 8), 0.0)
-        fold_z_ref[c] = folded(place(wz, low_z, CZ), place(sz, low_z, CZ))
-        pad = jnp.zeros((CZ - ROWS, WIDTH), F32)
-        fold_y_ref[c] = folded(
-            jnp.concatenate([rows_y_ref[:, at], pad], axis=0), jnp.concatenate([grads_y, pad], axis=0)
-        )
+        rims = jnp.concatenate([place(wz, rim_low, 8), place(sz, rim_low, 8)], axis=1)
+        rims = jnp.where(inside, rims, 0.0)
+        rest = rims - rims.astype(BF16).astype(F32)
+        zeros = jnp.zeros((104, 2 * WIDTH), F32)
+        fold_z_ref[c, 384:512] = jnp.concatenate([rims, rims, rest, zeros], axis=0).astype(BF16)
         return carry
 
     lax.fori_loop(0, frac_ref.shape[1] // WIDTH, step, 0)
 
 
-def stage(pot_ref, rim_ref, layers):
+def stage(pot_ref, layers):
+    lane = lax.broadcasted_iota(jnp.int32, (1, 128), 1)
+    strips = [layer[64:72] for layer in layers]
+    blank = [jnp.zeros((128 - 8 * len(layers), 128), F32)] if len(layers) < 16 else []
+    turned = jnp.concatenate(strips + blank, axis=0).T[:ROWS]
     for i, layer in enumerate(layers):
         high, low = halves(layer)
         at = pl.ds(i * ROWS, ROWS)
         pot_ref[at, 0:128] = high
         pot_ref[at, 128:256] = low
         pot_ref[at, 256:384] = high
-        at = pl.ds(i * 8, 8)
-        rim_ref[at, 0:128] = layer[64:72]
-    count = len(layers) * 8
-    high, low = halves(rim_ref[0:count, 0:128])
-    return jnp.concatenate([high, low, high], axis=1)
-
-
-def gather_part(first, last, cells, pot_ref, strips_ref, both_x_ref, rows_y_ref, grads_y_ref,
-                fold_z_ref, fold_y_ref, strip_ref, finish):
+        first, second, third = (pltpu.roll(turned, (128 + 8 * k - 8 * i) % 128, 1) for k in range(3))
+        value = jnp.where(lane < 8, first, jnp.where(lane < 16, second, third))
+        value = jnp.where(lane < 24, value, 0.0)
+        rounded = value.astype(BF16).astype(F32)
+        value = jnp.where((lane >= 8) & (lane < 16), value - rounded, rounded)
+        pot_ref[at, 384:512] = value.astype(BF16)
+
+
+def gather_part(cells, pot_ref, both_x_ref, rows_y_ref, grads_y_ref, fold_z_ref, finish):
     def one(c):
         at = pl.ds(pl.multiple_of(c * WIDTH, WIDTH), WIDTH)
         rows_y, grads_y = rows_y_ref[:, at], grads_y_ref[:, at]
-        rim_rows, rim_grads = strip_ref[0:8, at], strip_ref[8:16, at]
-        rims = dot(strips_ref[0 : len(cells) * 8], fold_y_ref[c])
         main = dot(pot_ref[0 : len(cells) * ROWS], fold_z_ref[c])
-        force_x = jnp.zeros((8, WIDTH), F32)
-        force_y = jnp.zeros((8, WIDTH), F32)
-        force_z = jnp.zeros((8, WIDTH), F32)
+        force_x = force_y = force_z = 0.0
         for i, x in enumerate(cells):
-            rim_plain = rims[i * 8 : i * 8 + 8, :WIDTH]
-            rim_sloped = rims[i * 8 : i * 8 + 8, WIDTH:]
-            sum_x = rim_rows * rim_plain
-            sum_y = rim_rows * rim_sloped
-            sum_z = rim_grads * rim_plain
+            sum_x = sum_y = sum_z = 0.0
             for y in range(ROWS // 8):
                 low = i * ROWS + y * 8
                 plain, sloped = main[low : low + 8, :WIDTH], main[low : low + 8, WIDTH:]
@@ -379,7 +381,7 @@
             one(i * UNROLL + u)
         return carry
 
-    lax.fori_loop(first // UNROLL, last // UNROLL, step, 0)
+    lax.fori_loop(0, fold_z_ref.shape[0] // UNROLL, step, 0)
 
 
 def turn_tables(to_kz_ref, to_ky_ref, to_kx_ref, from_kz_ref, from_ky_ref, from_kx_ref):
@@ -411,9 +413,9 @@
     total = len(INPUTS) + len(SMALL) + len(NAMES)
     hbm, out_ref, refs = refs[:total], refs[total], refs[total + 1 :]
     local, refs = refs[:total], refs[total:]
-    (rows_x_ref, rows_y_ref, both_z_ref, strips_ref, high_ref, low_ref, grid_ref, rim_in_ref, planes_ref,
-     send_ref, modes_ref, send2_ref, modes2_ref, blocks_ref, near_ref, far_ref, part_ref, pot_ref, rim_ref, strips2_ref,
-     both_x_ref, grads_y_ref, fold_z_ref, fold_y_ref, strip_ref, from_kz_ref, from_ky_ref, from_kx_ref,
+    (rows_x_ref, rows_y_ref, both_z_ref, strips_ref, both_y_ref, high_ref, low_ref, grid_ref, rim_in_ref, planes_ref,
+     send_ref, modes_ref, send2_ref, modes2_ref, blocks_ref, near_ref, far_ref, part_ref, pot_ref,
+     both_x_ref, grads_y_ref, fold_z_ref, from_kz_ref, from_ky_ref, from_kx_ref,
      load_sem, rim_send, rim_recv, a_send, a_recv, c_send, c_recv, d_send, d_recv,
      b_send, b_recv, e_send, e_recv) = refs
     loads = [pltpu.make_async_copy(h, v, load_sem.at[i]) for i, (h, v) in enumerate(zip(hbm, local))]
@@ -463,7 +465,9 @@
             load.start()
     spread = (rows_x_ref, rows_y_ref, both_z_ref, strips_ref)
     with jax.named_scope("rows"):
-        spread_rows(counts_ref, charges_ref, frac_ref, base_ref, *spread)
+        spread_rows(
+            counts_ref, charges_ref, frac_ref, base_ref, *spread, both_y_ref, high_ref, low_ref
+        )
     with jax.named_scope("spread4"):
         spread_group(4, *spread, high_ref, low_ref, grid_ref)
     def give(to):
@@ -542,9 +546,7 @@
             )
         spray(send2_ref, modes2_ref, d_send, d_recv, half)
     with jax.named_scope("gather_rows"):
-        gather_rows(
-            frac_ref, base_ref, rows_x_ref, both_x_ref, grads_y_ref, fold_z_ref, fold_y_ref, strip_ref, rows_y_ref
-        )
+        gather_rows(frac_ref, base_ref, rows_x_ref, both_x_ref, grads_y_ref, fold_z_ref)
     backward_kernel(
         modes2_ref, from_ky_ref, from_kz_ref, blocks_ref, functools.partial(arrive, modes2_ref, d_recv)
     )
@@ -555,12 +557,13 @@
         to = lax.rem(core + flip, 2) * 4 + lax.rem(height + up, 4)
         where = holder_of(to)
         theirs = ORDER_UP.index(((4 - up) % 4, flip))
-        copy = pltpu.make_async_remote_copy(
+        sends.append(pltpu.make_async_remote_copy(
             src_ref=blocks_ref.at[where["gz"] * 4 + where["gy"]], dst_ref=near_ref.at[theirs],
             send_sem=b_send.at[slot], recv_sem=b_recv.at[theirs], device_id=where, device_id_type=MESH,
-        )
+        ))
+
+    for copy in sends:
         copy.start()
-        sends.append(copy)
     near_ref[0] = blocks_ref[block]
     slot_cells = []
     for up, flip in ORDER_UP:
@@ -579,13 +582,15 @@
             send_sem=e_send.at[low_plane], recv_sem=e_recv.at[low_plane],
             device_id=before, device_id_type=MESH,
         )))
-    tools = (both_x_ref, rows_y_ref, grads_y_ref, fold_z_ref, fold_y_ref, strip_ref)
-    chunks = charges_ref.shape[1] // WIDTH
-
-    def keep(c, at, force_x, force_y, force_z):
-        part_ref[0, :, at] = force_x
-        part_ref[1, :, at] = force_y
-        part_ref[2, :, at] = force_z
+    tools = (both_x_ref, rows_y_ref, grads_y_ref, fold_z_ref)
+
+    def keep(c, at, *forces):
+        for d, force in enumerate(forces):
+            part_ref[d, :, at] = force
+
+    def add(c, at, *forces):
+        for d, force in enumerate(forces):
+            part_ref[d, :, at] += force
 
     def finish(c, at, *forces):
         slot = lax.broadcasted_iota(jnp.int32, (1, WIDTH), 1) + c * WIDTH
@@ -595,24 +600,31 @@
         ]
         out_ref[:, at] = -charge * jnp.concatenate(total, axis=0)
 
-    with jax.named_scope("bwait"):
-        for slot in range(1, EARLY):
+    def gather_slots(first, last, more, done):
+        layers = [near_ref[slot, i] for slot in range(first, last) for i in range(2)]
+        layers += [far_ref[i] for i in range(more)]
+        stage(pot_ref, layers)
+        cells = slot_cells[2 * first : 2 * last] + [CX + i for i in range(more)]
+        gather_part(cells, pot_ref, *tools, done)
+
+    with jax.named_scope("bwait1"):
+        drain(near_ref.at[1], b_recv.at[1])
+    with jax.named_scope("gather1"):
+        gather_slots(0, 2, 0, keep)
+    with jax.named_scope("bwait2"):
+        for slot in range(2, EARLY):
             drain(near_ref.at[slot], b_recv.at[slot])
         for slot, copy in rims_back:
             pl.when(slot < EARLY)(copy.start)
-    with jax.named_scope("stage1"):
-        strips2_ref[0 : EARLY * 16] = stage(
-            pot_ref, rim_ref, [near_ref[slot, i] for slot in range(EARLY) for i in range(2)]
-        )
-    with jax.named_scope("gather1"):
-        gather_part(0, chunks // 2, slot_cells[: 2 * EARLY], pot_ref, strips2_ref, *tools, keep)
-    with jax.named_scope("bwait2"):
+    with jax.named_scope("gather2"):
+        gather_slots(2, EARLY, 0, add)
+    with jax.named_scope("bwait3"):
         for slot in range(EARLY, COLUMN):
             drain(near_ref.at[slot], b_recv.at[slot])
         for slot, copy in rims_back:
             pl.when(slot >= EARLY)(copy.start)
-    with jax.named_scope("gather2"):
-        gather_part(chunks // 2, chunks, slot_cells[: 2 * EARLY], pot_ref, strips2_ref, *tools, keep)
+    with jax.named_scope("gather3"):
+        gather_slots(EARLY, COLUMN, 0, add)
     with jax.named_scope("sendwait"):
         rim.wait_send()
         for o in range(COLUMN):
@@ -629,13 +641,8 @@
         for _, copy in rims_back:
             copy.wait_send()
             copy.wait_recv()
-    with jax.named_scope("stage3"):
-        late = [near_ref[slot, i] for slot in range(EARLY, COLUMN) for i in range(2)]
-        late += [far_ref[i] for i in range(HALO)]
-        strips2_ref[0 : len(late) * 8] = stage(pot_ref, rim_ref, late)
-    with jax.named_scope("gather3"):
-        cells = slot_cells[2 * EARLY :] + [CX, CX + 1, CX + 2]
-        gather_part(0, chunks, cells, pot_ref, strips2_ref, *tools, finish)
+    with jax.named_scope("gather4"):
+        gather_slots(0, 0, HALO, finish)
 
 
 def per_device(charges, fractions, base_cells, counts):
@@ -654,6 +661,7 @@
         pltpu.VMEM((ROWS, atoms), F32),
         pltpu.VMEM((2 * CZ, atoms), BF16),
         pltpu.VMEM((160, CZ), F32),
+        pltpu.VMEM((2 * ROWS, atoms), BF16),
         pltpu.VMEM((4 * ROWS, atoms), BF16),
         pltpu.VMEM((4 * ROWS, atoms), BF16),
         pltpu.VMEM((20, ROWS, CZ), F32),
@@ -667,14 +675,10 @@
         pltpu.VMEM((COLUMN, 2, ROWS, CZ), F32),
         pltpu.VMEM((HALO, ROWS, CZ), F32),
         pltpu.VMEM((3, 8, atoms), F32),
-        pltpu.VMEM((2 * EARLY * ROWS, 384), BF16),
-        pltpu.VMEM((2 * EARLY * 8, 128), F32),
-        pltpu.VMEM((2 * EARLY * 8, 384), BF16),
+        pltpu.VMEM((2 * EARLY * ROWS, 512), BF16),
         pltpu.VMEM((atoms // WIDTH, 48, WIDTH), F32),
         pltpu.VMEM((ROWS, atoms), F32),
-        pltpu.VMEM((atoms // WIDTH, 384, 2 * WIDTH), BF16),
-        pltpu.VMEM((atoms // WIDTH, 384, 2 * WIDTH), BF16),
-        pltpu.VMEM((16, atoms), F32),
+        pltpu.VMEM((atoms // WIDTH, 512, 2 * WIDTH), BF16),
         pltpu.VMEM(t["to_kz"].shape, BF16),
         pltpu.VMEM(t["to_ky"].shape, BF16),
         pltpu.VMEM(t["to_kx"].shape, BF16),

time: 59.4 us -> 57.1 us (0.961)
  Pallas kernels: 56.6 us -> 54.9 us
    pallas_call x1, Pallas kernels: 56.6 us -> 54.9 us  [per_device(): pl.pallas_call(fused_kernel, out_shape=jax.ShapeDtypeStruct(fractions.sha...]
where the time goes in v4:
time: 57.1 us; the launch traced here: 56.9 us
  Pallas kernels  54.9 us (96%)
  local copies, waits for them, and re-layouts  1.38 us (2%)
  between operations  0.66 us (1%)
    pallas_call x1, Pallas kernels, per_device(): pl.pallas_call(fused_kernel, out_shape=jax.ShapeDtypeStruct(fractions.sha...  54.9 us
    unnamed x1, local copies, waits for them, and re-layouts  1.38 us

profile of v4, /device:TPU:1, one launch (start us, length us, event | category | flops | bytes accessed | tf_op | source)
XLA Modules:
  0.0 56.9 jit_solution(13587654261760086458)
XLA Ops:
  0.7 54.9 %shard_map.109 = f32[3,2048]{1,0:T(4,128)} custom-call(f32[1,2048]{1,0:T(1,128)} %bitcast.1, f32[3,2048]{1,0:T(4,128)} %refs_1_.1, s32[3,2048]{1,0:T(4,128)} %refs_2_.1, s32[1,1,1]{2,1,0:T(1,128)S(6)} %copy.13.refs_3_, f32[2,256]{1,0:T(2,128)} %constant.19.clone.refs_4_, bf16[2,256,256]{2,1,0:T(8,128)(2,1)} %constant.14.clone.refs_5_, ...), custom_call_target="tpu_custom_call" | custom-call | tf_op jit(solution)/shard_map/pallas_call | solution.py:688
  55.5 1.4 %copy.14 = f32[3,2048]{1,0:T(4,128)} copy(f32[3,2048]{1,0:T(4,128)} %shard_map.109) | data formatting | bytes 49152

commit v5 on v4

--- a/solution.py
+++ b/solution.py
@@ -219,10 +219,22 @@
         leave(half)
 
 
-def middle_kernel(part, data_ref, to_kx_ref, from_kx_ref, twist_ref, of_x_ref, of_z_ref, of_y_ref, out_ref):
+def fill_green(of_x_ref, of_z_ref, of_y_ref, green_ref):
     ix, iy, iz = block_index()
     mine = ix * COLUMN + plane_of(iz, iy)
     half, group = mine // 64, mine % 64
+    of_z = of_z_ref[half]
+    scale_xz = of_x_ref[0] * of_z[0:1]
+    square_xz = of_x_ref[1] + of_z[1:2]
+    for i in range(4):
+        ky = group * 4 + i
+        square = square_xz + of_y_ref[1, ky]
+        green_ref[i] = jnp.where(
+            square > 0.0, scale_xz * of_y_ref[0, ky] / jnp.maximum(square, 1.0), 0.0
+        )
+
+
+def middle_kernel(part, data_ref, to_kx_ref, from_kx_ref, twist_ref, green_ref, out_ref):
     lane = lax.broadcasted_iota(jnp.int32, (1, 128), 1)
     sign = jnp.where(lane < 64, 1.0, -1.0)
     flat = data_ref.reshape(2, 512, 128)
@@ -235,9 +247,6 @@
     )
     out = dot3(part_of(to_kx_ref), halves(both))
     cos, sin = twist_ref[0], twist_ref[1]
-    of_z = of_z_ref[half]
-    scale_xz = of_x_ref[0] * of_z[0:1]
-    square_xz = of_x_ref[1] + of_z[1:2]
     reals, imags = [], []
     for i in range(2):
         real = out[:128, i * 128 : (i + 1) * 128]
@@ -245,9 +254,7 @@
         real, imag = real * cos + imag * sin, imag * cos - real * sin
         real = real * sign + pltpu.roll(real, 64, 1)
         imag = imag * sign + pltpu.roll(imag, 64, 1)
-        ky = group * 4 + part * 2 + i
-        square = square_xz + of_y_ref[1, ky]
-        green = jnp.where(square > 0.0, scale_xz * of_y_ref[0, ky] / jnp.maximum(square, 1.0), 0.0)
+        green = green_ref[part * 2 + i]
         real, imag = real * green, imag * green
         real = real * sign + pltpu.roll(real, 64, 1)
         imag = imag * sign + pltpu.roll(imag, 64, 1)
@@ -264,7 +271,7 @@
             flat[part, pl.ds(c * 2 + i, 128, stride=4), :] = out[c * 128 : (c + 1) * 128, i * 128 : (i + 1) * 128]
 
 
-def backward_kernel(data_ref, from_ky_ref, from_kz_ref, out_ref, arrive):
+def backward_kernel(data_ref, from_ky_ref, from_kz_ref, out_ref, arrive, leave):
     lane = lax.broadcasted_iota(jnp.int32, (1, 128), 1)
     row = lax.broadcasted_iota(jnp.int32, (8, 128), 0)
     lower = lane < 64
@@ -299,6 +306,7 @@
                 out_ref[iz * 4 + iy, x, 64:72, :] = jnp.where(
                     row < HALO, near[after * 64 : after * 64 + 8], pltpu.roll(strip, HALO, 0)
                 )
+        leave(x)
 
 
 WIDTH = 128
@@ -415,7 +423,7 @@
     local, refs = refs[:total], refs[total:]
     (rows_x_ref, rows_y_ref, both_z_ref, strips_ref, both_y_ref, high_ref, low_ref, grid_ref, rim_in_ref, planes_ref,
      send_ref, modes_ref, send2_ref, modes2_ref, blocks_ref, near_ref, far_ref, part_ref, pot_ref,
-     both_x_ref, grads_y_ref, fold_z_ref, from_kz_ref, from_ky_ref, from_kx_ref,
+     both_x_ref, grads_y_ref, fold_z_ref, green_ref, from_kz_ref, from_ky_ref, from_kx_ref,
      load_sem, rim_send, rim_recv, a_send, a_recv, c_send, c_recv, d_send, d_recv,
      b_send, b_recv, e_send, e_recv) = refs
     loads = [pltpu.make_async_copy(h, v, load_sem.at[i]) for i, (h, v) in enumerate(zip(hbm, local))]
@@ -457,7 +465,12 @@
         pl.semaphore_signal(barrier, inc=1, device_id=where, device_id_type=MESH)
 
     with jax.named_scope("greet"):
-        everyone(greet)
+        for a, b in FAR:
+            to_x = lax.rem(lax.div(ix, 4) + a, 4) * 4 + lax.rem(lax.rem(ix, 4) + b, 4)
+            for _, where in others:
+                greet(None, {"gx": to_x, **where})
+        for _, where in others[:-1]:
+            greet(None, where)
     with jax.named_scope("load"):
         for load in loads[:first]:
             load.wait()
@@ -486,11 +499,15 @@
         spread_group(group_at(0), *spread, high_ref, low_ref, grid_ref)
     with jax.named_scope("barwait"):
         pl.semaphore_wait(barrier, 127)
-    rim = pltpu.make_async_remote_copy(
-        src_ref=grid_ref.at[pl.ds(CX, HALO)], dst_ref=rim_in_ref, send_sem=rim_send, recv_sem=rim_recv,
-        device_id=after, device_id_type=MESH,
-    )
-    rim.start()
+    rims = [
+        pltpu.make_async_remote_copy(
+            src_ref=grid_ref.at[pl.ds(CX + i, n)], dst_ref=rim_in_ref.at[pl.ds(i, n)],
+            send_sem=rim_send.at[i], recv_sem=rim_recv.at[i], device_id=after, device_id_type=MESH,
+        )
+        for i, n in ((0, 2), (2, 1))
+    ]
+    for rim in rims:
+        rim.start()
     give(2 * group_at(0))
     give(2 * group_at(0) + 1)
 
@@ -506,9 +523,11 @@
     with jax.named_scope("spread0"):
         spread_group(0, *spread, high_ref, low_ref, grid_ref)
     with jax.named_scope("rimwait"):
-        rim.wait_recv()
-    grid_ref[0:HALO] += rim_in_ref[...]
+        rims[0].wait_recv()
+    grid_ref[0:2] += rim_in_ref[0:2]
     give(0)
+    rims[1].wait_recv()
+    grid_ref[2] += rim_in_ref[2]
     give(1)
     planes_ref[pl.ds(block, 1)] = grid_ref[pl.ds(2 * plane, 2)].reshape(1, 2, ROWS, CZ)
     with jax.named_scope("await"):
@@ -537,33 +556,35 @@
         functools.partial(spray, send_ref, modes_ref, c_send, c_recv),
     )
     with jax.named_scope("turn"):
+        fill_green(t["of_x"], t["of_z"], of_y_ref, green_ref)
         turn_tables(t["to_kz"], t["to_ky"], t["to_kx"], from_kz_ref, from_ky_ref, from_kx_ref)
     for half in range(2):
         arrive(modes_ref, c_recv, half)
         with jax.named_scope("middle"):
             middle_kernel(
-                half, modes_ref, t["to_kx"], from_kx_ref, t["twist"], t["of_x"], t["of_z"], of_y_ref, send2_ref
+                half, modes_ref, t["to_kx"], from_kx_ref, t["twist"], green_ref, send2_ref
             )
         spray(send2_ref, modes2_ref, d_send, d_recv, half)
     with jax.named_scope("gather_rows"):
         gather_rows(frac_ref, base_ref, rows_x_ref, both_x_ref, grads_y_ref, fold_z_ref)
+    def give_back(x):
+        for slot in range(1, COLUMN if x else EARLY):
+            up, flip = ORDER_UP[slot]
+            to = lax.rem(core + flip, 2) * 4 + lax.rem(height + up, 4)
+            where = holder_of(to)
+            source = blocks_ref.at[where["gz"] * 4 + where["gy"]]
+            target = near_ref.at[ORDER_UP.index(((4 - up) % 4, flip))]
+            if slot < EARLY:
+                source, target = source.at[x], target.at[x]
+            pltpu.make_async_remote_copy(
+                src_ref=source, dst_ref=target, send_sem=b_send.at[slot],
+                recv_sem=b_recv.at[ORDER_UP.index(((4 - up) % 4, flip))], device_id=where, device_id_type=MESH,
+            ).start()
+
     backward_kernel(
-        modes2_ref, from_ky_ref, from_kz_ref, blocks_ref, functools.partial(arrive, modes2_ref, d_recv)
-    )
-
-    sends = []
-    for slot in range(1, COLUMN):
-        up, flip = ORDER_UP[slot]
-        to = lax.rem(core + flip, 2) * 4 + lax.rem(height + up, 4)
-        where = holder_of(to)
-        theirs = ORDER_UP.index(((4 - up) % 4, flip))
-        sends.append(pltpu.make_async_remote_copy(
-            src_ref=blocks_ref.at[where["gz"] * 4 + where["gy"]], dst_ref=near_ref.at[theirs],
-            send_sem=b_send.at[slot], recv_sem=b_recv.at[theirs], device_id=where, device_id_type=MESH,
-        ))
-
-    for copy in sends:
-        copy.start()
+        modes2_ref, from_ky_ref, from_kz_ref, blocks_ref, functools.partial(arrive, modes2_ref, d_recv),
+        give_back,
+    )
     near_ref[0] = blocks_ref[block]
     slot_cells = []
     for up, flip in ORDER_UP:
@@ -623,10 +644,9 @@
             drain(near_ref.at[slot], b_recv.at[slot])
         for slot, copy in rims_back:
             pl.when(slot >= EARLY)(copy.start)
-    with jax.named_scope("gather3"):
-        gather_slots(EARLY, COLUMN, 0, add)
     with jax.named_scope("sendwait"):
-        rim.wait_send()
+        for rim in rims:
+            rim.wait_send()
         for o in range(COLUMN):
             @pl.when(o != plane)
             def _():
@@ -635,14 +655,27 @@
         for half in range(2):
             drain(send_ref.at[half, pl.ds(0, 127)], c_send.at[half])
             drain(send2_ref.at[half, pl.ds(0, 127)], d_send.at[half])
-        for copy in sends:
-            copy.wait_send()
-    with jax.named_scope("ewait"):
-        for _, copy in rims_back:
-            copy.wait_send()
-            copy.wait_recv()
-    with jax.named_scope("gather4"):
+        for slot in range(1, COLUMN):
+            drain(blocks_ref.at[slot], b_send.at[slot])
+
+    def rims_home():
+        with jax.named_scope("ewait"):
+            for _, copy in rims_back:
+                copy.wait_recv()
+
+    @pl.when(height < 2)
+    def _():
+        rims_home()
+        gather_slots(EARLY, COLUMN, HALO, finish)
+
+    @pl.when(height >= 2)
+    def _():
+        gather_slots(EARLY, COLUMN, 0, add)
+        rims_home()
         gather_slots(0, 0, HALO, finish)
+
+    for _, copy in rims_back:
+        copy.wait_send()
 
 
 def per_device(charges, fractions, base_cells, counts):
@@ -679,10 +712,11 @@
         pltpu.VMEM((atoms // WIDTH, 48, WIDTH), F32),
         pltpu.VMEM((ROWS, atoms), F32),
         pltpu.VMEM((atoms // WIDTH, 512, 2 * WIDTH), BF16),
+        pltpu.VMEM((4, 128, 128), F32),
         pltpu.VMEM(t["to_kz"].shape, BF16),
         pltpu.VMEM(t["to_ky"].shape, BF16),
         pltpu.VMEM(t["to_kx"].shape, BF16),
-        dma((len(arrays),)), dma, dma, dma((COLUMN,)), dma((COLUMN,)), dma((2,)), dma((2,)), dma((2,)), dma((2,)),
+        dma((len(arrays),)), dma((HALO,)), dma((HALO,)), dma((COLUMN,)), dma((COLUMN,)), dma((2,)), dma((2,)), dma((2,)), dma((2,)),
         dma((COLUMN,)), dma((COLUMN,)), dma((2,)), dma((2,)),
     ]
     return pl.pallas_call(

time: 57.1 us -> 55.9 us (0.979)
  Pallas kernels: 54.9 us -> 53.7 us
    pallas_call x1, Pallas kernels: 54.9 us -> 53.7 us  [per_device(): pl.pallas_call(fused_kernel, out_shape=jax.ShapeDtypeStruct(fractions.sha...]
where the time goes in v5:
time: 55.9 us; the launch traced here: 55.8 us
  Pallas kernels  53.7 us (96%)
  local copies, waits for them, and re-layouts  1.38 us (2%)
  between operations  0.66 us (1%)
    pallas_call x1, Pallas kernels, per_device(): pl.pallas_call(fused_kernel, out_shape=jax.ShapeDtypeStruct(fractions.sha...  53.7 us
    unnamed x1, local copies, waits for them, and re-layouts  1.38 us

profile of v5, /device:TPU:1, one launch (start us, length us, event | category | flops | bytes accessed | tf_op | source)
XLA Modules:
  0.0 55.8 jit_solution(2994149015986651055)
XLA Ops:
  0.7 53.7 %shard_map.109 = f32[3,2048]{1,0:T(4,128)} custom-call(f32[1,2048]{1,0:T(1,128)} %bitcast.1, f32[3,2048]{1,0:T(4,128)} %refs_1_.1, s32[3,2048]{1,0:T(4,128)} %refs_2_.1, s32[1,1,1]{2,1,0:T(1,128)S(6)} %copy.13.refs_3_, f32[2,256]{1,0:T(2,128)} %constant.19.clone.refs_4_, bf16[2,256,256]{2,1,0:T(8,128)(2,1)} %constant.14.clone.refs_5_, ...), custom_call_target="tpu_custom_call" | custom-call | tf_op jit(solution)/shard_map/pallas_call | solution.py:722
  54.4 1.4 %copy.14 = f32[3,2048]{1,0:T(4,128)} copy(f32[3,2048]{1,0:T(4,128)} %shard_map.109) | data formatting | bytes 49152

commit v6 on v5

--- a/solution.py
+++ b/solution.py
@@ -310,7 +310,7 @@
 
 
 WIDTH = 128
-UNROLL = 4
+UNROLL = 16
 ORDER_UP = ((0, 0), (0, 1), (1, 0), (1, 1), (3, 0), (3, 1), (2, 0), (2, 1))
 EARLY = 6
 
@@ -425,7 +425,7 @@
      send_ref, modes_ref, send2_ref, modes2_ref, blocks_ref, near_ref, far_ref, part_ref, pot_ref,
      both_x_ref, grads_y_ref, fold_z_ref, green_ref, from_kz_ref, from_ky_ref, from_kx_ref,
      load_sem, rim_send, rim_recv, a_send, a_recv, c_send, c_recv, d_send, d_recv,
-     b_send, b_recv, e_send, e_recv) = refs
+     b_send, b_recv, e_send, e_recv, direct_sem) = refs
     loads = [pltpu.make_async_copy(h, v, load_sem.at[i]) for i, (h, v) in enumerate(zip(hbm, local))]
     first = len(INPUTS) + len(SMALL)
     for load in loads[:first]:
@@ -492,6 +492,15 @@
                 device_id=holder_of(to), device_id_type=MESH,
             ).start()
 
+    def give_layer(to, i):
+        @pl.when(to != plane)
+        def _():
+            pltpu.make_async_remote_copy(
+                src_ref=grid_ref.at[2 * to + i], dst_ref=planes_ref.at[block, i],
+                send_sem=a_send.at[to], recv_sem=a_recv.at[block],
+                device_id=holder_of(to), device_id_type=MESH,
+            ).start()
+
     def group_at(i):
         return 1 + lax.rem(i + plane, 3)
 
@@ -501,10 +510,10 @@
         pl.semaphore_wait(barrier, 127)
     rims = [
         pltpu.make_async_remote_copy(
-            src_ref=grid_ref.at[pl.ds(CX + i, n)], dst_ref=rim_in_ref.at[pl.ds(i, n)],
+            src_ref=grid_ref.at[CX + i], dst_ref=rim_in_ref.at[i],
             send_sem=rim_send.at[i], recv_sem=rim_recv.at[i], device_id=after, device_id_type=MESH,
         )
-        for i, n in ((0, 2), (2, 1))
+        for i in range(HALO)
     ]
     for rim in rims:
         rim.start()
@@ -522,13 +531,12 @@
         lax.fori_loop(1, 3, some, 0)
     with jax.named_scope("spread0"):
         spread_group(0, *spread, high_ref, low_ref, grid_ref)
-    with jax.named_scope("rimwait"):
-        rims[0].wait_recv()
-    grid_ref[0:2] += rim_in_ref[0:2]
-    give(0)
-    rims[1].wait_recv()
-    grid_ref[2] += rim_in_ref[2]
-    give(1)
+    give_layer(1, 1)
+    for i in range(HALO):
+        with jax.named_scope("rimwait"):
+            rims[i].wait_recv()
+        grid_ref[i] += rim_in_ref[i]
+        give_layer(i // 2, i % 2)
     planes_ref[pl.ds(block, 1)] = grid_ref[pl.ds(2 * plane, 2)].reshape(1, 2, ROWS, CZ)
     with jax.named_scope("await"):
         for load in loads[first:]:
@@ -568,7 +576,7 @@
     with jax.named_scope("gather_rows"):
         gather_rows(frac_ref, base_ref, rows_x_ref, both_x_ref, grads_y_ref, fold_z_ref)
     def give_back(x):
-        for slot in range(1, COLUMN if x else EARLY):
+        for slot in range(EARLY, COLUMN) if x is None else range(1, EARLY):
             up, flip = ORDER_UP[slot]
             to = lax.rem(core + flip, 2) * 4 + lax.rem(height + up, 4)
             where = holder_of(to)
@@ -628,22 +636,44 @@
         cells = slot_cells[2 * first : 2 * last] + [CX + i for i in range(more)]
         gather_part(cells, pot_ref, *tools, done)
 
+    direct = []
+    for low_plane, layers in ((0, 2), (1, 1)):
+        for flip in range(2):
+            far_z, far_y = low_plane % 2, 2 + flip
+            direct.append((low_plane, pltpu.make_async_remote_copy(
+                src_ref=blocks_ref.at[far_z * 4 + far_y, pl.ds(0, layers)],
+                dst_ref=far_ref.at[pl.ds(2 * low_plane, layers)], send_sem=direct_sem.at[flip],
+                recv_sem=e_recv.at[low_plane], device_id={**before, "gz": far_z, "gy": far_y},
+                device_id_type=MESH,
+            )))
+
+    def give_far():
+        for low_plane, copy in direct:
+            pl.when(plane == low_plane)(copy.start)
+        give_back(None)
+
     with jax.named_scope("bwait1"):
         drain(near_ref.at[1], b_recv.at[1])
+        for slot, copy in rims_back:
+            pl.when(slot < 2)(copy.start)
     with jax.named_scope("gather1"):
         gather_slots(0, 2, 0, keep)
+        give_far()
     with jax.named_scope("bwait2"):
         for slot in range(2, EARLY):
             drain(near_ref.at[slot], b_recv.at[slot])
         for slot, copy in rims_back:
-            pl.when(slot < EARLY)(copy.start)
+            pl.when((slot >= 2) & (slot < EARLY))(copy.start)
     with jax.named_scope("gather2"):
         gather_slots(2, EARLY, 0, add)
     with jax.named_scope("bwait3"):
         for slot in range(EARLY, COLUMN):
             drain(near_ref.at[slot], b_recv.at[slot])
-        for slot, copy in rims_back:
-            pl.when(slot >= EARLY)(copy.start)
+    with jax.named_scope("ewait"):
+        for _, copy in rims_back:
+            copy.wait_recv()
+    with jax.named_scope("gather3"):
+        gather_slots(EARLY, COLUMN, HALO, finish)
     with jax.named_scope("sendwait"):
         for rim in rims:
             rim.wait_send()
@@ -658,24 +688,10 @@
         for slot in range(1, COLUMN):
             drain(blocks_ref.at[slot], b_send.at[slot])
 
-    def rims_home():
-        with jax.named_scope("ewait"):
-            for _, copy in rims_back:
-                copy.wait_recv()
-
-    @pl.when(height < 2)
-    def _():
-        rims_home()
-        gather_slots(EARLY, COLUMN, HALO, finish)
-
-    @pl.when(height >= 2)
-    def _():
-        gather_slots(EARLY, COLUMN, 0, add)
-        rims_home()
-        gather_slots(0, 0, HALO, finish)
-
-    for _, copy in rims_back:
-        copy.wait_send()
+    for slot, copy in rims_back:
+        pl.when(slot < EARLY)(copy.wait_send)
+    for low_plane, copy in direct:
+        pl.when(plane == low_plane)(copy.wait_send)
 
 
 def per_device(charges, fractions, base_cells, counts):
@@ -717,7 +733,7 @@
         pltpu.VMEM(t["to_ky"].shape, BF16),
         pltpu.VMEM(t["to_kx"].shape, BF16),
         dma((len(arrays),)), dma((HALO,)), dma((HALO,)), dma((COLUMN,)), dma((COLUMN,)), dma((2,)), dma((2,)), dma((2,)), dma((2,)),
-        dma((COLUMN,)), dma((COLUMN,)), dma((2,)), dma((2,)),
+        dma((COLUMN,)), dma((COLUMN,)), dma((2,)), dma((2,)), dma((2,)),
     ]
     return pl.pallas_call(
         fused_kernel,

time: 55.9 us -> 54.6 us (0.977)
  Pallas kernels: 53.7 us -> 52.4 us
    pallas_call x1, Pallas kernels: 53.7 us -> 52.4 us  [per_device(): pl.pallas_call(fused_kernel, out_shape=jax.ShapeDtypeStruct(fractions.sha...]
where the time goes in v6:
time: 54.6 us; the launch traced here: 54.5 us
  Pallas kernels  52.4 us (96%)
  local copies, waits for them, and re-layouts  1.38 us (3%)
  between operations  0.66 us (1%)
    pallas_call x1, Pallas kernels, per_device(): pl.pallas_call(fused_kernel, out_shape=jax.ShapeDtypeStruct(fractions.sha...  52.4 us
    unnamed x1, local copies, waits for them, and re-layouts  1.38 us

profile of v6, /device:TPU:1, one launch (start us, length us, event | category | flops | bytes accessed | tf_op | source)
XLA Modules:
  0.0 54.5 jit_solution(4003282442197820752)
XLA Ops:
  0.7 52.4 %shard_map.109 = f32[3,2048]{1,0:T(4,128)} custom-call(f32[1,2048]{1,0:T(1,128)} %bitcast.1, f32[3,2048]{1,0:T(4,128)} %refs_1_.1, s32[3,2048]{1,0:T(4,128)} %refs_2_.1, s32[1,1,1]{2,1,0:T(1,128)S(6)} %copy.13.refs_3_, f32[2,256]{1,0:T(2,128)} %constant.19.clone.refs_4_, bf16[2,256,256]{2,1,0:T(8,128)(2,1)} %constant.14.clone.refs_5_, ...), custom_call_target="tpu_custom_call" | custom-call | tf_op jit(solution)/shard_map/pallas_call | solution.py:738
  53.1 1.4 %copy.14 = f32[3,2048]{1,0:T(4,128)} copy(f32[3,2048]{1,0:T(4,128)} %shard_map.109) | data formatting | bytes 49152
